TPU v7x, 16 devices: a whole 2x2x2 slice. The times are simulated.
16 devices in a mesh: ep: 16 (over z, y, x, core).
Axes of the slice: x: 2, y: 2, z: 2, core: 2. Of those that a mesh axis runs over, the one named last changes fastest.
Arguments:
- tokens: bfloat16 [2048, 4096], P('ep')
- k_cache: bfloat16 [2048, 256, 4, 128], P('ep')
- v_cache: bfloat16 [2048, 256, 4, 128], P('ep')
- positions: int32 [2048], P('ep')
- expert_one: int32 [2048], P('ep')
- expert_two: int32 [2048], P('ep')
- eligible: int32 [2048, 16], P('ep')
- ln1_gain: bfloat16 [4096], replicated
- ln1_bias: bfloat16 [4096], replicated
- w_query: bfloat16 [4096, 2048], replicated
- b_query: bfloat16 [2048], replicated
- w_key: bfloat16 [4096, 512], replicated
- b_key: bfloat16 [512], replicated
- w_value: bfloat16 [4096, 512], replicated
- b_value: bfloat16 [512], replicated
- w_out: bfloat16 [2048, 4096], replicated
- b_out: bfloat16 [4096], replicated
- ln2_gain: bfloat16 [4096], replicated
- ln2_bias: bfloat16 [4096], replicated
- w_router: bfloat16 [4096, 16], replicated
- w_gate: bfloat16 [16, 4096, 448], P('ep')
- w_up: bfloat16 [16, 4096, 448], P('ep')
- w_down: bfloat16 [16, 448, 4096], P('ep')
Outputs:
- output 1: bfloat16 [2048, 4096], P('ep')
- output 2: bfloat16 [2048, 4, 128], P('ep')
- output 3: bfloat16 [2048, 4, 128], P('ep')
All inputs are finite; a program needn't handle non-finite values.
Results may differ from a plain program's by a relative error of at most 0.00967011.
Values are sent between devices in bfloat16 or wider.
A program may use at most 1 GiB of HBM per device.

v0:
```python
import jax
import jax.numpy as jnp
from jax import lax
from jax.sharding import PartitionSpec as P

ROPE_BASE = 10000.0
LN_EPS = 1e-5


def layer_norm(values_in, gain, bias):
    mean_val = jnp.mean(values_in, axis=-1, keepdims=True)
    centered = values_in - mean_val
    var_val = jnp.mean(centered * centered, axis=-1, keepdims=True)
    return centered * lax.rsqrt(var_val + LN_EPS) * gain.astype(jnp.float32) + bias.astype(jnp.float32)


def rope_tables(positions, head_dim):
    half_dim = head_dim // 2
    inv_freq = ROPE_BASE ** (jnp.arange(half_dim, dtype=jnp.float32) * (-2.0 / head_dim))
    angles = positions.astype(jnp.float32)[:, None] * inv_freq[None, :]
    angles = jnp.concatenate([angles, angles], axis=-1)
    return jnp.cos(angles), jnp.sin(angles)


def apply_rope(values_in, cos_tab, sin_tab):
    half_dim = values_in.shape[-1] // 2
    rotated = jnp.concatenate([-values_in[..., half_dim:], values_in[..., :half_dim]], axis=-1)
    return values_in * cos_tab[:, None, :] + rotated * sin_tab[:, None, :]


def attention_block(tokens, k_cache, v_cache, positions, ln1_gain, ln1_bias, w_query, b_query, w_key, b_key, w_value, b_value, w_out, b_out):
    tok_count, seq_len, kv_heads, head_dim = k_cache.shape
    num_heads = w_query.shape[1] // head_dim
    group_size = num_heads // kv_heads
    x_f = tokens.astype(jnp.float32)
    h_one = layer_norm(x_f, ln1_gain, ln1_bias).astype(jnp.bfloat16)
    cos_tab, sin_tab = rope_tables(positions, head_dim)
    q_lin = jnp.dot(h_one, w_query, preferred_element_type=jnp.float32) + b_query.astype(jnp.float32)
    q_rot = apply_rope(q_lin.reshape(tok_count, num_heads, head_dim), cos_tab, sin_tab).astype(jnp.bfloat16)
    q_grp = q_rot.reshape(tok_count, kv_heads, group_size, head_dim)
    k_lin = jnp.dot(h_one, w_key, preferred_element_type=jnp.float32) + b_key.astype(jnp.float32)
    key_new = apply_rope(k_lin.reshape(tok_count, kv_heads, head_dim), cos_tab, sin_tab).astype(jnp.bfloat16)
    v_lin = jnp.dot(h_one, w_value, preferred_element_type=jnp.float32) + b_value.astype(jnp.float32)
    value_new = v_lin.astype(jnp.bfloat16).reshape(tok_count, kv_heads, head_dim)
    score_scale = head_dim ** -0.5
    s_cache = jnp.einsum('tkgd,tskd->tkgs', q_grp, k_cache, preferred_element_type=jnp.float32) * score_scale
    valid_mask = jnp.arange(seq_len)[None, None, None, :] < positions[:, None, None, None]
    s_cache = jnp.where(valid_mask, s_cache, -jnp.inf)
    s_new = jnp.einsum('tkgd,tkd->tkg', q_grp, key_new, preferred_element_type=jnp.float32) * score_scale
    top_val = jnp.maximum(jnp.max(s_cache, axis=-1), s_new)
    e_cache = jnp.exp(s_cache - top_val[..., None])
    e_new = jnp.exp(s_new - top_val)
    denom_sum = jnp.sum(e_cache, axis=-1) + e_new
    p_cache = (e_cache / denom_sum[..., None]).astype(jnp.bfloat16)
    p_new = (e_new / denom_sum).astype(jnp.bfloat16)
    attn_vals = jnp.einsum('tkgs,tskd->tkgd', p_cache, v_cache, preferred_element_type=jnp.float32)
    attn_vals = attn_vals + p_new.astype(jnp.float32)[..., None] * value_new.astype(jnp.float32)[:, :, None, :]
    attn_flat = attn_vals.astype(jnp.bfloat16).reshape(tok_count, num_heads * head_dim)
    x_mid = (x_f + jnp.dot(attn_flat, w_out, preferred_element_type=jnp.float32) + b_out.astype(jnp.float32)).astype(jnp.bfloat16)
    return x_mid, key_new, value_new


def router_gates(h_two, w_router, expert_one, expert_two, eligible):
    logits = jnp.dot(h_two, w_router, preferred_element_type=jnp.float32)
    expert_ids = jnp.arange(logits.shape[1])[None, :]
    hit_one = expert_ids == expert_one[:, None]
    hit_two = expert_ids == expert_two[:, None]
    keep_one = eligible == 1
    keep_two = keep_one & jnp.logical_not(hit_one)
    prob_one = jax.nn.softmax(jnp.where(keep_one, logits, -jnp.inf), axis=-1)
    prob_two = jax.nn.softmax(jnp.where(keep_two, logits, -jnp.inf), axis=-1)
    gate_one = jnp.sum(jnp.where(hit_one, prob_one, 0.0), axis=-1)
    gate_two = jnp.sum(jnp.where(hit_two, prob_two, 0.0), axis=-1)
    return gate_one, gate_two


def send_plan(expert_one, expert_two, local_experts, groups, tok_count):
    num_experts = local_experts * groups
    pair_expert = jnp.concatenate([expert_one, expert_two])
    token_ids = jnp.arange(tok_count, dtype=jnp.int32)
    pair_token = jnp.concatenate([token_ids, token_ids])
    one_hot = (pair_expert[:, None] == jnp.arange(num_experts, dtype=jnp.int32)[None, :]).astype(jnp.int32)
    pair_slot = jnp.sum(one_hot * jnp.cumsum(one_hot, axis=0), axis=1) - 1
    buffer_row = ((pair_expert % local_experts) * groups + pair_expert // local_experts) * tok_count + pair_slot
    src_token = jax.ops.segment_sum(pair_token, buffer_row, num_segments=num_experts * tok_count)
    return buffer_row, src_token


def expert_mlp(expert_in, w_gate, w_up, w_down):
    u_val = jnp.einsum('emd,edf->emf', expert_in, w_gate, preferred_element_type=jnp.float32)
    v_val = jnp.einsum('emd,edf->emf', expert_in, w_up, preferred_element_type=jnp.float32)
    z_val = (jax.nn.silu(u_val) * v_val).astype(jnp.bfloat16)
    return jnp.einsum('emf,efd->emd', z_val, w_down, preferred_element_type=jnp.float32).astype(jnp.bfloat16)


def solution(mesh):
    groups = mesh.shape['ep']

    def local_step(tokens, k_cache, v_cache, positions, expert_one, expert_two, eligible, ln1_gain, ln1_bias, w_query, b_query, w_key, b_key, w_value, b_value, w_out, b_out, ln2_gain, ln2_bias, w_router, w_gate, w_up, w_down):
        x_mid, key_new, value_new = attention_block(tokens, k_cache, v_cache, positions, ln1_gain, ln1_bias, w_query, b_query, w_key, b_key, w_value, b_value, w_out, b_out)
        h_two = layer_norm(x_mid.astype(jnp.float32), ln2_gain, ln2_bias).astype(jnp.bfloat16)
        gate_one, gate_two = router_gates(h_two, w_router, expert_one, expert_two, eligible)
        tok_count, d_model = h_two.shape
        local_experts = w_gate.shape[0]
        num_experts = local_experts * groups
        buffer_row, src_token = send_plan(expert_one, expert_two, local_experts, groups, tok_count)
        send_rows = jnp.take(h_two, src_token, axis=0).reshape(local_experts, groups, tok_count, d_model)
        recv_rows = lax.all_to_all(send_rows, 'ep', 1, 1, tiled=True)
        expert_in = recv_rows.reshape(local_experts, groups * tok_count, d_model)
        expert_out = expert_mlp(expert_in, w_gate, w_up, w_down)
        back_rows = lax.all_to_all(expert_out.reshape(local_experts, groups, tok_count, d_model), 'ep', 1, 1, tiled=True)
        back_flat = back_rows.reshape(num_experts * tok_count, d_model)
        out_one = jnp.take(back_flat, buffer_row[:tok_count], axis=0)
        out_two = jnp.take(back_flat, buffer_row[tok_count:], axis=0)
        y_sum = gate_one[:, None] * out_one.astype(jnp.float32) + gate_two[:, None] * out_two.astype(jnp.float32)
        tokens_out = (x_mid.astype(jnp.float32) + y_sum).astype(jnp.bfloat16)
        return tokens_out, key_new, value_new

    row_spec = P('ep', None)
    cache_spec = P('ep', None, None, None)
    vec_spec = P('ep')
    rep_one = P(None)
    rep_two = P(None, None)
    expert_spec = P('ep', None, None)
    in_specs = (row_spec, cache_spec, cache_spec, vec_spec, vec_spec, vec_spec, row_spec, rep_one, rep_one, rep_two, rep_one, rep_two, rep_one, rep_two, rep_one, rep_two, rep_one, rep_one, rep_one, rep_two, expert_spec, expert_spec, expert_spec)
    out_specs = (row_spec, expert_spec, expert_spec)
    return jax.shard_map(local_step, mesh=mesh, in_specs=in_specs, out_specs=out_specs, check_vma=False)
```

profile of v0, /device:TPU:0, one launch (start us, length us, event | category | flops | bytes accessed | tf_op | source)
XLA Modules:
  0.0 591.4 jit_solution(13138657287980424779)
XLA Ops:
  6.3 2.0 scatter_custom_fusion
  10.9 1.7 fusion.18
  12.7 8.2 %convolution_add_fusion.1 = f32[128,2048]{1,0:T(8,128)S(1)} fusion(bf16[4096,2048]{1,0:T(8,128)(2,1)} %param.34, f32[2048]{0:T(1024)S(1)} %convert_element_type.98, bf16[128,4096]{1,0:T(8,128)(2,1)S(1)} %copy-done.2, f32[4096]{0:T(1024)S(1)} %convert_element_type.96, f32[4096]{0:T(1024)S(1)} %convert_element_type.95, f32[128]{0:T(128)S(1)} %add_rsqrt_fusion.1, ...), kind=kOutput, calls=%fused_computation.24 | convolution fusion | flops 2150891520 | bytes 18916352 | tf_op jit(solution)/shard_map/dot_general | solution.py:38
  21.8 1.7 slice_negate_fusion
  29.7 15.4 %fusion.23 = (f32[128,4,4]{2,1,0:T(4,128)S(1)}, f32[128,4,4,256]{3,2,1,0:T(4,128)S(1)}) fusion(pred[128,256]{1,0:T(8,128)(4,1)} %iota_compare_fusion, bf16[128,4,4,128]{3,2,1,0:T(4,128)(2,1)} %copy-done.5, bf16[128,256,4,128]{3,2,1,0:T(4,128)(2,1)} %param.26), kind=kOutput, calls=%fused_computation.36 | convolution fusion | flops 135788544 | bytes 36216832 | tf_op jit(solution)/shard_map/tkgd,tskd->tkgs/dot_general | solution.py:46
  46.8 3.2 fusion.31
  50.0 1.7 copy.47
  56.7 3.6 fusion.30
  60.4 1.6 reshape.274
  62.0 1.6 convert_element_type.108
  63.6 15.7 %fusion.27 = bf16[128,4,4,128]{3,2,1,0:T(4,128)(2,1)} fusion(bf16[128,256,4,128]{3,2,1,0:T(4,128)(2,1)} %param.27, f32[128,4,4,256]{3,2,1,0:T(4,128)S(1)} %get-tuple-element.27, f32[128,4,4]{2,1,0:T(4,128)} %copy.48, f32[128,4,4]{2,1,0:T(4,128)S(1)} %copy.46, pred[128,256]{1,0:T(8,128)(4,1)} %iota_compare_fusion, f32[128,4,128]{2,1,0:T(4,128)} %convert_element_type.108, ...), kind=kOutput, calls=%fused_computation.38 | convolution fusion | flops 137625600 | bytes 36495360 | tf_op jit(solution)/shard_map/tkgs,tskd->tkgd/dot_general | solution.py:56
  79.3 2.2 reshape.275
  81.5 8.5 %fusion.68 = (f32[128]{0:T(128)S(1)}, f32[128,4096]{1,0:T(8,128)S(1)}) fusion(f32[4096]{0:T(1024)S(1)} %convert_element_type.110, bf16[128,2048]{1,0:T(8,128)(2,1)} %reshape.275, bf16[2048,4096]{1,0:T(8,128)(2,1)} %param.40, bf16[128,4096]{1,0:T(8,128)(2,1)S(1)} %copy-done.2), kind=kOutput, calls=%fused_computation.118 | convolution fusion | flops 2150629376 | bytes 20464128 | tf_op jit(solution)/shard_map/dot_general | solution.py:59
  91.2 14.3 %gather_fusion = bf16[2048,4096]{1,0:T(8,128)(2,1)} fusion(bf16[128,4096]{1,0:T(8,128)(2,1)S(1)} %add_convert_fusion.1, s32[2048]{0:T(1024)S(1)} %copy-done.7), kind=kCustom, calls=%fused_computation.2 | custom fusion | bytes 33562624 | tf_op jit(solution)/shard_map/jit(_take)/gather | solution.py:107
  105.5 8.5 %broadcast_select_fusion = bf16[1,16,128,4096]{3,2,0,1:T(8,128)(2,1)S(1)} fusion(bf16[1,16,128,4096]{3,2,0,1:T(8,128)(2,1)} %bitcast.75, pred[16,128]{1,0:T(8,128)(4,1)S(1)} %copy-done.11), kind=kLoop, calls=%fused_computation.8 | loop fusion | flops 8388608 | bytes 33556480 | tf_op jit(solution)/shard_map/jit(_take)/select_n | solution.py:107
  114.0 194.3 %all_to_all.10 = bf16[1,16,128,4096]{3,2,0,1:T(8,128)(2,1)S(1)} all-to-all(bf16[1,16,128,4096]{3,2,0,1:T(8,128)(2,1)S(1)} %broadcast_select_fusion), channel_id=1, replica_groups=mesh['ep'=16] {'ep'}, dimensions={1} | all-to-all | bytes 33554432 | tf_op jit(solution)/shard_map/all_to_all | solution.py:108
  308.3 5.7 copy-done.1
  314.0 9.6 %fusion.10 = f32[2048,448]{0,1:T(8,128)} fusion(bf16[2048,4096]{1,0:T(8,128)(2,1)S(1)} %bitcast.77, bf16[1,4096,448]{1,2,0:T(8,128)(2,1)S(1)} %copy-done.24), kind=kOutput, calls=%fused_computation.17 | convolution fusion | flops 7516192768 | bytes 24117248 | tf_op jit(solution)/shard_map/emd,edf->emf/dot_general | solution.py:90
  323.6 24.4 %convolution_convert_fusion = bf16[2048,4096]{1,0:T(8,128)(2,1)} fusion(bf16[1,448,4096]{2,1,0:T(8,128)(2,1)} %param.47, f32[2048,448]{0,1:T(8,128)} %fusion.10, bf16[2048,4096]{1,0:T(8,128)(2,1)} %bitcast.78, bf16[1,4096,448]{1,2,0:T(8,128)(2,1)} %param.46), kind=kOutput, calls=%fused_computation.9 | convolution fusion | flops 15046279168 | bytes 44564480 | tf_op jit(solution)/shard_map/emf,efd->emd/dot_general | solution.py:93
  348.0 13.9 %all-to-all-start.1 = ((bf16[1,16,128,4096]{3,2,0,1:T(8,128)(2,1)}), bf16[1,16,128,4096]{3,2,0,1:T(8,128)(2,1)}, u32[]{:S(2)}, u32[]{:S(2)}) async-start(bf16[1,16,128,4096]{3,2,0,1:T(8,128)(2,1)} %bitcast.76), calls=%async_computation.1 | async-start | bytes 33554432 | tf_op jit(solution)/shard_map/all_to_all | solution.py:111
  362.5 204.2 %all-to-all-done.1 = bf16[1,16,128,4096]{3,2,0,1:T(8,128)(2,1)} async-done(((bf16[1,16,128,4096]{3,2,0,1:T(8,128)(2,1)}), bf16[1,16,128,4096]{3,2,0,1:T(8,128)(2,1)}, u32[]{:S(2)}, u32[]{:S(2)}) %all-to-all-start.1) | async-done | bytes 16777248 | tf_op jit(solution)/shard_map/all_to_all | solution.py:111
  566.7 10.1 %gather_fusion.1 = bf16[128,4096]{1,0:T(8,128)(2,1)S(1)} fusion(bf16[2048,4096]{1,0:T(8,128)(2,1)} %bitcast.19, s32[1024]{0:T(1024)S(1)} %get-tuple-element.32), kind=kCustom, calls=%fused_computation.clone | custom fusion | bytes 2097664 | tf_op jit(solution)/shard_map/jit(_take)/gather | solution.py:113
  576.8 11.1 %gather_fusion.2 = bf16[128,4096]{1,0:T(8,128)(2,1)} fusion(bf16[2048,4096]{1,0:T(8,128)(2,1)} %bitcast.19, s32[1024]{0:T(1024)S(1)} %get-tuple-element.31), kind=kCustom, calls=%fused_computation.1.clone | custom fusion | bytes 2097664 | tf_op jit(solution)/shard_map/jit(_take)/gather | solution.py:114
  587.9 3.0 add_convert_fusion
  (107 shorter events, 23.7 us)
Async XLA Ops:
  0.6 361.4 %copy-start = (bf16[4096,16]{0,1:T(8,128)(2,1)S(1)}, bf16[4096,16]{0,1:T(8,128)(2,1)}, u32[]{:S(2)}) copy-start(bf16[4096,16]{0,1:T(8,128)(2,1)} %param.44) | copy-start | bytes 393220
  0.6 12.0 %copy-start.2 = (bf16[128,4096]{1,0:T(8,128)(2,1)S(1)}, bf16[128,4096]{1,0:T(8,128)(2,1)}, u32[]{:S(2)}) copy-start(bf16[128,4096]{1,0:T(8,128)(2,1)} %param.25) | copy-start | bytes 3145732
  0.7 11.9 %copy-start.12 = (bf16[4096]{0:T(1024)(128)(2,1)S(1)}, bf16[4096]{0:T(1024)(128)(2,1)}, u32[]{:S(2)}) copy-start(bf16[4096]{0:T(1024)(128)(2,1)} %param.32) | copy-start | bytes 24580
  0.7 11.9 %copy-start.13 = (bf16[4096]{0:T(1024)(128)(2,1)S(1)}, bf16[4096]{0:T(1024)(128)(2,1)}, u32[]{:S(2)}) copy-start(bf16[4096]{0:T(1024)(128)(2,1)} %param.33) | copy-start | bytes 24580
  0.7 11.9 %copy-start.18 = (bf16[2048]{0:T(1024)(128)(2,1)S(1)}, bf16[2048]{0:T(1024)(128)(2,1)}, u32[]{:S(2)}) copy-start(bf16[2048]{0:T(1024)(128)(2,1)} %param.35) | copy-start | bytes 12292
  10.9 13.0 %copy-start.22 = (f32[128]{0:T(128)}, f32[128]{0:T(128)S(1)}, u32[]{:S(2)}) copy-start(f32[128]{0:T(128)S(1)} %broadcast_multiply_fusion.2) | copy-start | bytes 1540
  12.6 11.3 %copy-start.25 = (f32[128]{0:T(128)}, f32[128]{0:T(128)S(1)}, u32[]{:S(2)}) copy-start(f32[128]{0:T(128)S(1)} %add_rsqrt_fusion.1) | copy-start | bytes 1540
  12.6 11.3 %copy-start.8 = (f32[4096]{0:T(1024)}, f32[4096]{0:T(1024)S(1)}, u32[]{:S(2)}) copy-start(f32[4096]{0:T(1024)S(1)} %convert_element_type.95) | copy-start | bytes 49156
  12.6 11.3 %copy-start.9 = (f32[4096]{0:T(1024)}, f32[4096]{0:T(1024)S(1)}, u32[]{:S(2)}) copy-start(f32[4096]{0:T(1024)S(1)} %convert_element_type.96) | copy-start | bytes 49156
  21.8 2.1 copy-start.21
  21.8 3.0 copy-start.23
  25.6 1.2 copy-start.3
  25.7 1.6 copy-start.4
  26.1 3.5 copy-start.6
  28.2 0.8 copy-start.5
  63.6 17.9 %copy-start.14 = (bf16[4096]{0:T(1024)(128)(2,1)S(1)}, bf16[4096]{0:T(1024)(128)(2,1)}, u32[]{:S(2)}) copy-start(bf16[4096]{0:T(1024)(128)(2,1)} %param.41) | copy-start | bytes 24580
  91.2 14.3 %copy-start.11 = (pred[16,128]{1,0:T(8,128)(4,1)S(1)}, pred[16,128]{1,0:T(8,128)(4,1)}, u32[]{:S(2)}) copy-start(pred[16,128]{1,0:T(8,128)(4,1)} %and_bitcast_fusion) | copy-start | bytes 6148
  114.0 200.0 %copy-start.24 = (bf16[1,4096,448]{1,2,0:T(8,128)(2,1)S(1)}, bf16[1,4096,448]{1,2,0:T(8,128)(2,1)}, u32[]{:S(2)}) copy-start(bf16[1,4096,448]{1,2,0:T(8,128)(2,1)} %param.45) | copy-start | bytes 11010052
  308.3 5.7 copy-start.1
  348.0 13.9 %copy-start.19 = (s32[256]{0:T(256)S(1)}, s32[256]{0:T(256)}, u32[]{:S(2)}) copy-start(s32[256]{0:T(256)} %get-tuple-element.24) | copy-start | bytes 3076
  348.0 14.0 %copy-start.10 = (s32[128,16]{0,1:T(8,128)S(1)}, s32[128,16]{0,1:T(8,128)}, u32[]{:S(2)}) copy-start(s32[128,16]{0,1:T(8,128)} %param.31) | copy-start | bytes 24580
  348.0 14.4 %copy-start.17 = (s32[128]{0:T(128)S(1)}, s32[128]{0:T(128)}, u32[]{:S(2)}) copy-start(s32[128]{0:T(128)} %param.29) | copy-start | bytes 1540
  348.0 14.5 %copy-start.20 = (s32[128]{0:T(128)S(1)}, s32[128]{0:T(128)}, u32[]{:S(2)}) copy-start(s32[128]{0:T(128)} %param.30) | copy-start | bytes 1540
  348.0 218.7 %all-to-all-start.1 = ((bf16[1,16,128,4096]{3,2,0,1:T(8,128)(2,1)}), bf16[1,16,128,4096]{3,2,0,1:T(8,128)(2,1)}, u32[]{:S(2)}, u32[]{:S(2)}) async-start(bf16[1,16,128,4096]{3,2,0,1:T(8,128)(2,1)} %bitcast.76), calls=%async_computation.1 | async-start | bytes 33554432 | tf_op jit(solution)/shard_map/all_to_all | solution.py:111
  (3 other events, 2.2 us)
where the time goes:
time: 599 us; the launch traced here: 591 us
  waiting for transfers between devices  204 us (34%)
  blocking collectives  194 us (32%)
  matrix products  87.3 us (15%)
  local copies, waits for them, and re-layouts  56.5 us (9%)
  other arithmetic  33.6 us (6%)
  starting transfers between devices  13.9 us (2%)
    all_to_all x1, waiting for transfers between devices, local_step(): lax.all_to_all(expert_out.reshape(local_experts, groups, tok_count, d_mod...  204 us
    all_to_all x1, blocking collectives, local_step(): recv_rows = lax.all_to_all(send_rows, 'ep', 1, 1, tiled=True)  194 us
    dot_general x1, matrix products, expert_mlp(): jnp.einsum('emf,efd->emd', z_val, w_down, preferred_element_type=jnp.floa...  24.4 us
    dot_general x1, matrix products, attention_block(): jnp.einsum('tkgs,tskd->tkgd', p_cache, v_cache, preferred_element_type=jn...  15.7 us
    dot_general x1, matrix products, attention_block(): jnp.einsum('tkgd,tskd->tkgs', q_grp, k_cache, preferred_element_type=jnp....  15.4 us
    gather x1, local copies, waits for them, and re-layouts, local_step(): jnp.take(h_two, src_token, axis=0)  14.3 us
    all_to_all x1, starting transfers between devices, local_step(): lax.all_to_all(expert_out.reshape(local_experts, groups, tok_count, d_mod...  13.9 us
  transfers between devices with their start and end apart: 1, of which 1 were waited for; matrix products, arithmetic and copies ran while one was open for 0% of the time, Pallas kernels for 0%

commit v1 on v0

--- a/solution.py
+++ b/solution.py
@@ -74,18 +74,6 @@
     return gate_one, gate_two
 
 
-def send_plan(expert_one, expert_two, local_experts, groups, tok_count):
-    num_experts = local_experts * groups
-    pair_expert = jnp.concatenate([expert_one, expert_two])
-    token_ids = jnp.arange(tok_count, dtype=jnp.int32)
-    pair_token = jnp.concatenate([token_ids, token_ids])
-    one_hot = (pair_expert[:, None] == jnp.arange(num_experts, dtype=jnp.int32)[None, :]).astype(jnp.int32)
-    pair_slot = jnp.sum(one_hot * jnp.cumsum(one_hot, axis=0), axis=1) - 1
-    buffer_row = ((pair_expert % local_experts) * groups + pair_expert // local_experts) * tok_count + pair_slot
-    src_token = jax.ops.segment_sum(pair_token, buffer_row, num_segments=num_experts * tok_count)
-    return buffer_row, src_token
-
-
 def expert_mlp(expert_in, w_gate, w_up, w_down):
     u_val = jnp.einsum('emd,edf->emf', expert_in, w_gate, preferred_element_type=jnp.float32)
     v_val = jnp.einsum('emd,edf->emf', expert_in, w_up, preferred_element_type=jnp.float32)
@@ -103,16 +91,15 @@
         tok_count, d_model = h_two.shape
         local_experts = w_gate.shape[0]
         num_experts = local_experts * groups
-        buffer_row, src_token = send_plan(expert_one, expert_two, local_experts, groups, tok_count)
-        send_rows = jnp.take(h_two, src_token, axis=0).reshape(local_experts, groups, tok_count, d_model)
-        recv_rows = lax.all_to_all(send_rows, 'ep', 1, 1, tiled=True)
-        expert_in = recv_rows.reshape(local_experts, groups * tok_count, d_model)
-        expert_out = expert_mlp(expert_in, w_gate, w_up, w_down)
-        back_rows = lax.all_to_all(expert_out.reshape(local_experts, groups, tok_count, d_model), 'ep', 1, 1, tiled=True)
-        back_flat = back_rows.reshape(num_experts * tok_count, d_model)
-        out_one = jnp.take(back_flat, buffer_row[:tok_count], axis=0)
-        out_two = jnp.take(back_flat, buffer_row[tok_count:], axis=0)
-        y_sum = gate_one[:, None] * out_one.astype(jnp.float32) + gate_two[:, None] * out_two.astype(jnp.float32)
+        me = lax.axis_index('ep')
+        all_rows = lax.all_gather(h_two, 'ep', axis=0, tiled=True)
+        all_experts = lax.all_gather(jnp.stack([expert_one, expert_two], axis=1), 'ep', axis=0, tiled=True)
+        expert_out = expert_mlp(all_rows[None], w_gate, w_up, w_down)[0]
+        mine = (all_experts == me)[:, :, None]
+        slots = jnp.where(mine, expert_out[:, None, :], jnp.zeros((), jnp.bfloat16))
+        slots = slots.reshape(groups, tok_count, 2, d_model).transpose(0, 2, 1, 3).reshape(groups * 2 * tok_count, d_model)
+        back = lax.psum_scatter(slots, 'ep', scatter_dimension=0, tiled=True)
+        y_sum = gate_one[:, None] * back[:tok_count].astype(jnp.float32) + gate_two[:, None] * back[tok_count:].astype(jnp.float32)
         tokens_out = (x_mid.astype(jnp.float32) + y_sum).astype(jnp.bfloat16)
         return tokens_out, key_new, value_new
 

time: 599 us -> 580 us (0.968); the launches traced: 591 us -> 579 us
  waiting for transfers between devices: 204 us -> 409 us
  blocking collectives: 194 us -> 14.5 us
  local copies, waits for them, and re-layouts: 56.5 us -> 12.4 us
  starting transfers between devices: 13.9 us -> 0.08 us
  between operations: 1.59 us -> 14.5 us
    reduce_scatter x0 -> x1, waiting for transfers between devices: none -> 344 us  [local_step(): back = lax.psum_scatter(slots, 'ep', scatter_dimension=0, tiled=True)]
    all_to_all x1 -> x0, waiting for transfers between devices: 204 us -> none  [local_step(): lax.all_to_all(expert_out.reshape(local_experts, groups, tok_count, d_mod...]
    all_to_all x1 -> x0, blocking collectives: 194 us -> none  [local_step(): recv_rows = lax.all_to_all(send_rows, 'ep', 1, 1, tiled=True)]
    all_gather x0 -> x1, waiting for transfers between devices: none -> 64.5 us  [local_step(): all_rows = lax.all_gather(h_two, 'ep', axis=0, tiled=True)]
    gather x3 -> x0, local copies, waits for them, and re-layouts: 35.5 us -> none  [the longest x1 14.3 us: local_step(): jnp.take(h_two, src_token, axis=0)]
    all_gather x0 -> x1, blocking collectives: none -> 14.5 us  [local_step(): lax.all_gather(jnp.stack([expert_one, expert_two], axis=1), 'ep', axis=0,...]
    all_to_all x1 -> x0, starting transfers between devices: 13.9 us -> none  [local_step(): lax.all_to_all(expert_out.reshape(local_experts, groups, tok_count, d_mod...]
    select_n x1, other arithmetic: 8.48 us -> 15.9 us  [local_step(): slots = jnp.where(mine, expert_out[:, None, :], jnp.zeros((), jnp.bfloat16))]
  transfers between devices with their start and end apart: 1 -> 2, of which waited for: 1 -> 2; matrix products, arithmetic and copies ran while one was open for 0% -> 0% of each run, Pallas kernels for 0% -> 0%
where the time goes in v1:
time: 580 us; the launch traced here: 579 us
  waiting for transfers between devices  409 us (71%)
  matrix products  92.8 us (16%)
  other arithmetic  35.8 us (6%)
  blocking collectives  14.5 us (2%)
  between operations  14.5 us (2%)
  local copies, waits for them, and re-layouts  12.4 us (2%)
    reduce_scatter x1, waiting for transfers between devices, local_step(): back = lax.psum_scatter(slots, 'ep', scatter_dimension=0, tiled=True)  344 us
    all_gather x1, waiting for transfers between devices, local_step(): all_rows = lax.all_gather(h_two, 'ep', axis=0, tiled=True)  64.5 us
    dot_general x1, matrix products, expert_mlp(): jnp.einsum('emf,efd->emd', z_val, w_down, preferred_element_type=jnp.floa...  24.3 us
    select_n x1, other arithmetic, local_step(): slots = jnp.where(mine, expert_out[:, None, :], jnp.zeros((), jnp.bfloat16))  15.9 us
    dot_general x1, matrix products, attention_block(): jnp.einsum('tkgs,tskd->tkgd', p_cache, v_cache, preferred_element_type=jn...  15.7 us
    dot_general x1, matrix products, attention_block(): jnp.einsum('tkgd,tskd->tkgs', q_grp, k_cache, preferred_element_type=jnp....  15.4 us
    all_gather x1, blocking collectives, local_step(): lax.all_gather(jnp.stack([expert_one, expert_two], axis=1), 'ep', axis=0,...  14.5 us
    dot_general x1, matrix products, expert_mlp(): jnp.einsum('emd,edf->emf', expert_in, w_gate, preferred_element_type=jnp....  13.7 us
  transfers between devices with their start and end apart: 2, of which 2 were waited for; matrix products, arithmetic and copies ran while one was open for 0% of the time, Pallas kernels for 0%

profile of v1, /device:TPU:0, one launch (start us, length us, event | category | flops | bytes accessed | tf_op | source)
XLA Modules:
  0.0 578.7 jit_solution(1837693667227161327)
XLA Ops:
  8.1 1.3 iota_compare_fusion
  9.4 1.5 convert_reduce_fusion
  10.9 1.7 fusion.18
  14.9 2.9 fusion.30
  17.9 3.0 convolution_add_fusion.3
  21.9 8.2 %convolution_add_fusion.1 = f32[128,2048]{1,0:T(8,128)S(1)} fusion(bf16[4096,2048]{1,0:T(8,128)(2,1)} %param.32, f32[2048]{0:T(1024)S(1)} %convert_element_type.93, bf16[128,4096]{1,0:T(8,128)(2,1)S(1)} %copy-done.1, f32[4096]{0:T(1024)S(1)} %convert_element_type.91, f32[4096]{0:T(1024)S(1)} %convert_element_type.90, f32[128]{0:T(128)S(1)} %add_rsqrt_fusion.1, ...), kind=kOutput, calls=%fused_computation.20 | convolution fusion | flops 2150891520 | bytes 18916352 | tf_op jit(solution)/shard_map/dot_general | solution.py:38
  30.1 1.7 reshape.186
  35.0 15.4 %fusion.23 = (f32[128,4,4]{2,1,0:T(4,128)S(1)}, f32[128,4,4,256]{3,2,1,0:T(4,128)S(1)}) fusion(pred[128,256]{1,0:T(8,128)(4,1)} %iota_compare_fusion, bf16[128,4,4,128]{3,2,1,0:T(4,128)(2,1)} %copy-done.5, bf16[128,256,4,128]{3,2,1,0:T(4,128)(2,1)} %param.24), kind=kOutput, calls=%fused_computation.32 | convolution fusion | flops 135788544 | bytes 36216832 | tf_op jit(solution)/shard_map/tkgd,tskd->tkgs/dot_general | solution.py:46
  52.0 3.2 fusion.31
  55.2 1.7 copy.40
  56.8 1.3 fusion.52
  58.2 1.5 copy.43
  59.7 1.5 copy.41
  61.3 15.7 %fusion.27 = bf16[128,4,4,128]{3,2,1,0:T(4,128)(2,1)} fusion(bf16[128,256,4,128]{3,2,1,0:T(4,128)(2,1)} %param.25, f32[128,4,4,256]{3,2,1,0:T(4,128)S(1)} %get-tuple-element.18, f32[128,4,4]{2,1,0:T(4,128)} %copy.41, f32[128,4,4]{2,1,0:T(4,128)S(1)} %copy.39, pred[128,256]{1,0:T(8,128)(4,1)} %iota_compare_fusion, f32[128,4,128]{2,1,0:T(4,128)} %convert_element_type.103, ...), kind=kOutput, calls=%fused_computation.34 | convolution fusion | flops 137625600 | bytes 36495360 | tf_op jit(solution)/shard_map/tkgs,tskd->tkgd/dot_general | solution.py:56
  76.9 2.2 reshape.190
  79.2 8.5 %fusion.61 = (f32[128]{0:T(128)S(1)}, f32[128,4096]{1,0:T(8,128)S(1)}) fusion(f32[4096]{0:T(1024)S(1)} %copy-done.9, bf16[128,2048]{1,0:T(8,128)(2,1)} %reshape.190, bf16[2048,4096]{1,0:T(8,128)(2,1)} %param.38, bf16[128,4096]{1,0:T(8,128)(2,1)S(1)} %copy-done.1), kind=kOutput, calls=%fused_computation.90 | convolution fusion | flops 2150629376 | bytes 20464128 | tf_op jit(solution)/shard_map/dot_general | solution.py:59
  88.4 1.4 add_convert_fusion.1
  89.9 14.5 %all_gather.6 = s32[2048,2]{0,1:T(2,128)S(1)} all-gather(s32[128,2]{0,1:T(2,128)S(1)} %pad_add_fusion), channel_id=1, replica_groups=mesh['ep'=16] {'ep'}, dimensions={0}, use_global_device_ids=true | all-gather | bytes 17408 | tf_op jit(solution)/shard_map/all_gather | solution.py:96
  104.4 64.5 %all-gather.2.cloned.1.call-done = bf16[2048,4096]{1,0:T(8,128)(2,1)} async-done(((bf16[128,4096]{1,0:T(8,128)(2,1)}), bf16[2048,4096]{1,0:T(8,128)(2,1)}) %all-gather.2.cloned.1.call-update) | async-done | bytes 16777232 | tf_op jit(solution)/shard_map/all_gather | solution.py:95
  168.9 13.7 %fusion.10 = f32[2048,448]{0,1:T(8,128)} fusion(bf16[2048,4096]{1,0:T(8,128)(2,1)} %all-gather.2.cloned.1.call-done, bf16[1,4096,448]{1,2,0:T(8,128)(2,1)} %param.43), kind=kOutput, calls=%fused_computation.13 | convolution fusion | flops 7516192768 | bytes 24117248 | tf_op jit(solution)/shard_map/emd,edf->emf/dot_general | solution.py:78
  182.6 24.3 %convolution_convert_fusion = bf16[2048,4096]{1,0:T(8,128)(2,1)} fusion(bf16[1,448,4096]{2,1,0:T(8,128)(2,1)} %param.45, f32[2048,448]{0,1:T(8,128)} %fusion.10, bf16[2048,4096]{1,0:T(8,128)(2,1)} %all-gather.2.cloned.1.call-done, bf16[1,4096,448]{1,2,0:T(8,128)(2,1)} %param.44), kind=kOutput, calls=%fused_computation.5 | convolution fusion | flops 15046279168 | bytes 44564480 | tf_op jit(solution)/shard_map/emf,efd->emd/dot_general | solution.py:81
  206.9 15.9 %bitcast_select_fusion = bf16[4096,4096]{1,0:T(8,128)(2,1)} fusion(pred[4096]{0:T(1024)(128)(4,1)S(1)} %broadcast_in_dim.95, bf16[16,128,4096]{2,1,0:T(8,128)(2,1)} %bitcast.54), kind=kLoop, calls=%fused_computation | loop fusion | flops 16777216 | bytes 50335744 | tf_op jit(solution)/shard_map/jit(_where)/select_n | solution.py:99
  224.5 344.3 %reduce-scatter.2.cloned.1.call-done = bf16[256,4096]{1,0:T(8,128)(2,1)} async-done(((bf16[4096,4096]{1,0:T(8,128)(2,1)}), bf16[256,4096]{1,0:T(8,128)(2,1)}) %reduce-scatter.2.cloned.1.call-update) | async-done | bytes 2097168 | tf_op jit(solution)/shard_map/reduce_scatter | solution.py:101
  568.8 3.1 add_convert_fusion
  (83 shorter events, 11.3 us)
Async XLA Ops:
  7.2 215.7 %copy-start = (bf16[4096,16]{0,1:T(8,128)(2,1)S(1)}, bf16[4096,16]{0,1:T(8,128)(2,1)}, u32[]{:S(2)}) copy-start(bf16[4096,16]{0,1:T(8,128)(2,1)} %param.42) | copy-start | bytes 393220
  7.2 7.7 %copy-start.1 = (bf16[128,4096]{1,0:T(8,128)(2,1)S(1)}, bf16[128,4096]{1,0:T(8,128)(2,1)}, u32[]{:S(2)}) copy-start(bf16[128,4096]{1,0:T(8,128)(2,1)} %param.23) | copy-start | bytes 3145732
  7.2 5.3 copy-start.19
  7.2 5.4 copy-start.20
  7.2 5.4 copy-start.17
  7.2 5.4 copy-start.11
  7.2 5.4 copy-start.12
  7.2 5.4 copy-start.13
  7.3 6.0 %copy-start.14 = (bf16[4096]{0:T(1024)(128)(2,1)S(1)}, bf16[4096]{0:T(1024)(128)(2,1)}, u32[]{:S(2)}) copy-start(bf16[4096]{0:T(1024)(128)(2,1)} %param.40) | copy-start | bytes 24580
  7.3 6.6 %copy-start.15 = (bf16[4096]{0:T(1024)(128)(2,1)S(1)}, bf16[4096]{0:T(1024)(128)(2,1)}, u32[]{:S(2)}) copy-start(bf16[4096]{0:T(1024)(128)(2,1)} %param.41) | copy-start | bytes 24580
  7.3 161.6 %all-gather.2.cloned.1.call-start = ((), (), s32[]{:S(2)}) async-start(), calls=%async_computation.1 | async-start | bytes 17825792 | tf_op jit(solution)/shard_map/all_gather | solution.py:95
  17.9 3.1 copy-start.4
  32.0 1.2 copy-start.3
  32.6 2.2 copy-start.6
  34.1 0.8 copy-start.5
  61.3 17.9 %copy-start.9 = (f32[4096]{0:T(1024)S(1)}, f32[4096]{0:T(1024)}, u32[]{:S(2)}) copy-start(f32[4096]{0:T(1024)} %convert_element_type.105) | copy-start | bytes 49156
  87.7 0.7 copy-start.7
  87.7 0.7 copy-start.8
  88.4 1.5 copy-start.16
  88.4 1.5 copy-start.18
  89.8 479.0 %reduce-scatter.2.cloned.1.call-start = ((), (), s32[]{:S(2)}) async-start(), calls=%async_computation.2 | async-start | bytes 35651584 | tf_op jit(solution)/shard_map/reduce_scatter | solution.py:101
  222.8 1.2 copy-start.2
  222.8 1.2 copy-start.10
Sparse Core Ops, SparseCore 0:
  90.0 78.9 all-gather.1
  223.0 345.8 reduce-scatter.1

commit v2 on v1

--- a/solution.py
+++ b/solution.py
@@ -1,6 +1,10 @@
+import functools
+
 import jax
 import jax.numpy as jnp
 from jax import lax
+from jax.experimental import pallas as pl
+from jax.experimental.pallas import tpu as pltpu
 from jax.sharding import PartitionSpec as P
 
 ROPE_BASE = 10000.0
@@ -74,33 +78,295 @@
     return gate_one, gate_two
 
 
-def expert_mlp(expert_in, w_gate, w_up, w_down):
-    u_val = jnp.einsum('emd,edf->emf', expert_in, w_gate, preferred_element_type=jnp.float32)
-    v_val = jnp.einsum('emd,edf->emf', expert_in, w_up, preferred_element_type=jnp.float32)
-    z_val = (jax.nn.silu(u_val) * v_val).astype(jnp.bfloat16)
-    return jnp.einsum('emf,efd->emd', z_val, w_down, preferred_element_type=jnp.float32).astype(jnp.bfloat16)
+MESH = pl.DeviceIdType.MESH
+ORDERS = ((1, 2, 4), (2, 4, 1), (4, 1, 2))
+LANES = 128
+WIDTH = 256
+
+
+def flip(me, bit):
+    return me + bit - 2 * bit * ((me // bit) % 2)
+
+
+def meet_neighbours():
+    me = lax.axis_index('ep')
+    barrier = pltpu.get_barrier_semaphore()
+    for bit in (1, 2, 4, 8):
+        pl.semaphore_signal(barrier, inc=1, device_id=(flip(me, bit),), device_id_type=MESH)
+    pl.semaphore_wait(barrier, 4)
+    return me
+
+
+def gather_kernel(bounds, h_ref, wg_ref, wu_ref, z_ref, id_ref, x_a, x_b, x_c, own_sem, send_sem, recv_sem, side_send, side_recv):
+    rows = x_a.shape[1] // 2
+    bufs = (x_a, x_b, x_c)
+    copies = []
+    for f in range(3):
+        lo, hi = bounds[f]
+        copies.append(pltpu.make_async_copy(h_ref.at[:, pl.ds(lo, hi - lo)], bufs[f].at[0, pl.ds(0, rows)], own_sem.at[f]))
+        copies[-1].start()
+    me = meet_neighbours()
+
+    def hop(f, src, bit):
+        return pltpu.make_async_remote_copy(
+            src_ref=bufs[f].at[src, pl.ds(0, rows)], dst_ref=bufs[f].at[src ^ bit, pl.ds(0, rows)],
+            send_sem=send_sem.at[f, src ^ bit], recv_sem=recv_sem.at[f, src ^ bit],
+            device_id=(flip(me, 2 * bit),), device_id_type=MESH)
+
+    def side(f, src):
+        return pltpu.make_async_remote_copy(
+            src_ref=bufs[f].at[src, pl.ds(0, rows)], dst_ref=bufs[f].at[src, pl.ds(rows, rows)],
+            send_sem=side_send.at[f, src], recv_sem=side_recv.at[f, src],
+            device_id=(flip(me, 1),), device_id_type=MESH)
+
+    def landed(f, slot):
+        hop(f, 0, slot).wait_recv()
+
+    def activate(pair):
+        u_val = v_val = None
+        for f in range(3):
+            lo, hi = bounds[f]
+            hi = min(hi, wg_ref.shape[0])
+            x_val = bufs[f][pair, :, : hi - lo]
+            u_part = jnp.dot(x_val, wg_ref[lo:hi, :], preferred_element_type=jnp.float32)
+            v_part = jnp.dot(x_val, wu_ref[lo:hi, :], preferred_element_type=jnp.float32)
+            u_val = u_part if u_val is None else u_val + u_part
+            v_val = v_part if v_val is None else v_val + v_part
+        z_ref[pair] = (jax.nn.silu(u_val) * v_val).astype(jnp.bfloat16)
+        id_ref[pair] = bufs[2][pair, :, pl.ds(bounds[2][1] - bounds[2][0] - LANES, LANES)]
+
+    for f in range(3):
+        copies[f].wait()
+        hop(f, 0, ORDERS[f][0]).start()
+    for f in range(3):
+        side(f, 0).start()
+    for stage in (1, 2):
+        for f in range(3):
+            hop(f, 0, ORDERS[f][stage]).start()
+    for f in range(3):
+        side(f, 0).wait_recv()
+    activate(0)
+    for f in range(3):
+        a, b, g = ORDERS[f]
+        landed(f, a)
+        hop(f, a, b).start()
+        hop(f, a, g).start()
+        side(f, a).start()
+    for f in range(3):
+        a, b, g = ORDERS[f]
+        landed(f, b)
+        hop(f, b, g).start()
+        side(f, b).start()
+    for f in range(3):
+        a, b, g = ORDERS[f]
+        landed(f, a ^ b)
+        hop(f, a ^ b, g).start()
+        side(f, a ^ b).start()
+    for f in range(3):
+        g = ORDERS[f][2]
+        landed(f, g)
+        side(f, g).start()
+    for f in range(3):
+        for slot in (1, 2, 4):
+            side(f, slot).wait_recv()
+
+    @pl.loop(0, 3)
+    def _(i):
+        activate(i * (i + 1) // 2 + 1)
+
+    for f in range(3):
+        a, b, g = ORDERS[f]
+        landed(f, a ^ g)
+        side(f, a ^ g).start()
+        landed(f, b ^ g)
+        side(f, b ^ g).start()
+    for f in range(3):
+        for slot in (3, 5, 6):
+            side(f, slot).wait_recv()
+
+    @pl.loop(0, 3)
+    def _(i):
+        activate(6 - i * (i + 1) // 2)
+
+    for f in range(3):
+        landed(f, 7)
+        side(f, 7).start()
+    for f in range(3):
+        side(f, 7).wait_recv()
+    activate(7)
+    for f in range(3):
+        for slot in range(8):
+            side(f, slot).wait_send()
+        for slot in range(1, 8):
+            hop(f, 0, slot).wait_send()
+
+
+def return_kernel(z_ref, wd_ref, rel_ref, gate_ref, x_ref, out_ref, pair_buf, side_buf, near_buf, turn_buf, turn_in, last_buf, last_in, side_send, side_recv, hop_send, hop_recv):
+    rows = x_ref.shape[0]
+    chunks = pair_buf.shape[0]
+    me = meet_neighbours()
+
+    def slot_of(f, place):
+        a, b, g = ORDERS[f]
+        return a * (place // 4) + b * (place // 2 % 2) + g * (place % 2)
+
+    def remote(src, dst, send, recv, bit):
+        return pltpu.make_async_remote_copy(src_ref=src, dst_ref=dst, send_sem=send, recv_sem=recv, device_id=(flip(me, bit),), device_id_type=MESH)
+
+    def side(q):
+        return remote(side_buf.at[q], pair_buf.at[q, 1], side_send.at[q], side_recv.at[q], 1)
+
+    def hop_one(f, q):
+        return remote(pair_buf.at[q, :, pl.ds(4 * rows, 4 * rows)], near_buf.at[q], hop_send.at[0, q], hop_recv.at[0, q], 2 * ORDERS[f][0])
+
+    def hop_two(f, q):
+        return remote(turn_buf.at[q], turn_in.at[q], hop_send.at[1, q], hop_recv.at[1, q], 2 * ORDERS[f][1])
+
+    def hop_three(f, q):
+        return remote(last_buf.at[q], last_in.at[q], hop_send.at[2, q], hop_recv.at[2, q], 2 * ORDERS[f][2])
+
+    def project(f, q):
+        w_val = wd_ref[:, pl.ds(pl.multiple_of(q * WIDTH, WIDTH), WIDTH)]
+        for place in range(8):
+            e_val = jnp.dot(z_ref[slot_of(f, place)], w_val, preferred_element_type=jnp.float32).astype(jnp.bfloat16)
+            pair_buf[q, 0, place * rows:(place + 1) * rows, :] = e_val[:rows]
+            side_buf[q, place * rows:(place + 1) * rows, :] = e_val[rows:]
+        side(q).start()
+
+    def send_far(f, q):
+        side(q).wait_recv()
+        hop_one(f, q).start()
+
+    def choose(f, q, place, k, other):
+        rel = rel_ref[slot_of(f, place)][:, k:k + 1]
+        at = pl.ds(place * rows, rows)
+        far = 2 * ORDERS[f][0]
+        val = other
+        if val is None:
+            val = near_buf[q, 1, at, :].astype(jnp.float32)
+        else:
+            val = jnp.where(rel == far + 1, near_buf[q, 1, at, :].astype(jnp.float32), val)
+        val = jnp.where(rel == far, near_buf[q, 0, at, :].astype(jnp.float32), val)
+        val = jnp.where(rel == 1, pair_buf[q, 1, at, :].astype(jnp.float32), val)
+        return jnp.where(rel == 0, pair_buf[q, 0, at, :].astype(jnp.float32), val)
+
+    def turn(f, q):
+        hop_one(f, q).wait_recv()
+        for k in range(2):
+            for half in range(2):
+                turn_buf[q, k, half * rows:(half + 1) * rows, :] = choose(f, q, 2 + half, k, None).astype(jnp.bfloat16)
+        hop_two(f, q).start()
+
+    def last(f, q):
+        hop_two(f, q).wait_recv()
+        for k in range(2):
+            other = turn_in[q, k, rows:2 * rows, :].astype(jnp.float32)
+            last_buf[q, k] = choose(f, q, 1, k, other).astype(jnp.bfloat16)
+        hop_three(f, q).start()
+
+    def finish(f, q):
+        hop_three(f, q).wait_recv()
+        g_bit = 2 * ORDERS[f][2]
+        y_val = None
+        for k in range(2):
+            rel = rel_ref[0][:, k:k + 1]
+            other = jnp.where((rel // g_bit) % 2 == 1, last_in[q, k].astype(jnp.float32), turn_in[q, k, :rows, :].astype(jnp.float32))
+            part = gate_ref[:, k:k + 1] * choose(f, q, 0, k, other)
+            y_val = part if y_val is None else y_val + part
+        at = pl.ds(pl.multiple_of(q * WIDTH, WIDTH), WIDTH)
+        out_ref[:, at] = (x_ref[:, at].astype(jnp.float32) + y_val).astype(jnp.bfloat16)
+
+    def sweep(step):
+        @pl.loop(0, chunks // 3)
+        def _(j):
+            for f in range(3):
+                step(f, 3 * j + f)
+        for q in range(chunks // 3 * 3, chunks):
+            step(q % 3, q)
+
+    for f in range(3):
+        project(f, f)
+
+    @pl.loop(1, chunks // 3)
+    def _(j):
+        for f in range(3):
+            project(f, 3 * j + f)
+            send_far(f, 3 * j + f - 3)
+
+    for q in range(chunks // 3 * 3, chunks):
+        project(q % 3, q)
+    for f in range(3):
+        send_far(f, chunks // 3 * 3 - 3 + f)
+    for q in range(chunks // 3 * 3, chunks):
+        send_far(q % 3, q)
+    sweep(turn)
+    sweep(last)
+    sweep(finish)
+
+    def drain(f, q):
+        side(q).wait_send()
+        hop_one(f, q).wait_send()
+        hop_two(f, q).wait_send()
+        hop_three(f, q).wait_send()
+    sweep(drain)
+
+
+def gather_and_activate(h_two, expert_one, expert_two, w_gate, w_up):
+    rows, d_model = h_two.shape
+    d_ff = w_gate.shape[1]
+    ids = jnp.pad(jnp.stack([expert_one, expert_two], axis=1).astype(jnp.bfloat16), ((0, 0), (0, LANES - 2)))
+    h_ext = jnp.concatenate([h_two, ids], axis=1)
+    tiles = (d_model + LANES) // LANES
+    cuts = [LANES * ((tiles * f + 2) // 3) for f in range(4)]
+    bounds = tuple((cuts[f], cuts[f + 1]) for f in range(3))
+    vmem = pl.BlockSpec(memory_space=pltpu.VMEM)
+    return pl.pallas_call(
+        functools.partial(gather_kernel, bounds),
+        name='gather_rows',
+        out_shape=(jax.ShapeDtypeStruct((8, 2 * rows, d_ff), jnp.bfloat16), jax.ShapeDtypeStruct((8, 2 * rows, LANES), jnp.bfloat16)),
+        in_specs=[pl.BlockSpec(memory_space=pl.ANY), vmem, vmem],
+        out_specs=(vmem, vmem),
+        scratch_shapes=[pltpu.VMEM((8, 2 * rows, hi - lo), jnp.bfloat16) for lo, hi in bounds] + [
+            pltpu.SemaphoreType.DMA((3,)),
+            pltpu.SemaphoreType.DMA((3, 8)), pltpu.SemaphoreType.DMA((3, 8)),
+            pltpu.SemaphoreType.DMA((3, 8)), pltpu.SemaphoreType.DMA((3, 8))],
+        compiler_params=pltpu.CompilerParams(collective_id=0, has_side_effects=True, vmem_limit_bytes=60 * 1024 * 1024),
+    )(h_ext, w_gate, w_up)
+
+
+def project_and_return(z_val, w_down, rel, gates, x_mid):
+    rows, d_model = x_mid.shape
+    chunks = d_model // WIDTH
+    vmem = pl.BlockSpec(memory_space=pltpu.VMEM)
+    return pl.pallas_call(
+        return_kernel,
+        name='return_rows',
+        out_shape=jax.ShapeDtypeStruct((rows, d_model), jnp.bfloat16),
+        in_specs=[vmem] * 5,
+        out_specs=vmem,
+        scratch_shapes=[
+            pltpu.VMEM((chunks, 2, 8 * rows, WIDTH), jnp.bfloat16),
+            pltpu.VMEM((chunks, 8 * rows, WIDTH), jnp.bfloat16),
+            pltpu.VMEM((chunks, 2, 4 * rows, WIDTH), jnp.bfloat16),
+            pltpu.VMEM((chunks, 2, 2 * rows, WIDTH), jnp.bfloat16),
+            pltpu.VMEM((chunks, 2, 2 * rows, WIDTH), jnp.bfloat16),
+            pltpu.VMEM((chunks, 2, rows, WIDTH), jnp.bfloat16),
+            pltpu.VMEM((chunks, 2, rows, WIDTH), jnp.bfloat16),
+            pltpu.SemaphoreType.DMA((chunks,)), pltpu.SemaphoreType.DMA((chunks,)),
+            pltpu.SemaphoreType.DMA((3, chunks)), pltpu.SemaphoreType.DMA((3, chunks))],
+        compiler_params=pltpu.CompilerParams(collective_id=1, has_side_effects=True, vmem_limit_bytes=63 * 1024 * 1024),
+    )(z_val, w_down, rel, gates, x_mid)
 
 
 def solution(mesh):
-    groups = mesh.shape['ep']
-
     def local_step(tokens, k_cache, v_cache, positions, expert_one, expert_two, eligible, ln1_gain, ln1_bias, w_query, b_query, w_key, b_key, w_value, b_value, w_out, b_out, ln2_gain, ln2_bias, w_router, w_gate, w_up, w_down):
         x_mid, key_new, value_new = attention_block(tokens, k_cache, v_cache, positions, ln1_gain, ln1_bias, w_query, b_query, w_key, b_key, w_value, b_value, w_out, b_out)
         h_two = layer_norm(x_mid.astype(jnp.float32), ln2_gain, ln2_bias).astype(jnp.bfloat16)
         gate_one, gate_two = router_gates(h_two, w_router, expert_one, expert_two, eligible)
-        tok_count, d_model = h_two.shape
-        local_experts = w_gate.shape[0]
-        num_experts = local_experts * groups
-        me = lax.axis_index('ep')
-        all_rows = lax.all_gather(h_two, 'ep', axis=0, tiled=True)
-        all_experts = lax.all_gather(jnp.stack([expert_one, expert_two], axis=1), 'ep', axis=0, tiled=True)
-        expert_out = expert_mlp(all_rows[None], w_gate, w_up, w_down)[0]
-        mine = (all_experts == me)[:, :, None]
-        slots = jnp.where(mine, expert_out[:, None, :], jnp.zeros((), jnp.bfloat16))
-        slots = slots.reshape(groups, tok_count, 2, d_model).transpose(0, 2, 1, 3).reshape(groups * 2 * tok_count, d_model)
-        back = lax.psum_scatter(slots, 'ep', scatter_dimension=0, tiled=True)
-        y_sum = gate_one[:, None] * back[:tok_count].astype(jnp.float32) + gate_two[:, None] * back[tok_count:].astype(jnp.float32)
-        tokens_out = (x_mid.astype(jnp.float32) + y_sum).astype(jnp.bfloat16)
+        z_val, ids = gather_and_activate(h_two, expert_one, expert_two, w_gate[0], w_up[0])
+        rel = ids[:, :h_two.shape[0]].astype(jnp.int32) ^ lax.axis_index('ep')
+        gates = jnp.pad(jnp.stack([gate_one, gate_two], axis=1), ((0, 0), (0, LANES - 2)))
+        tokens_out = project_and_return(z_val, w_down[0], rel, gates, x_mid)
         return tokens_out, key_new, value_new
 
     row_spec = P('ep', None)

time: 580 us -> 305 us (0.53)
  waiting for transfers between devices: 409 us -> 0 us
  Pallas kernels: 0 us -> 201 us
  matrix products: 92.8 us -> 55.5 us
  other arithmetic: 35.8 us -> 19.6 us
  blocking collectives: 14.5 us -> 0 us
  local copies, waits for them, and re-layouts: 12.4 us -> 26.6 us
  between operations: 14.5 us -> 1.15 us
    reduce_scatter x1 -> x0, waiting for transfers between devices: 344 us -> none  [local_step(): back = lax.psum_scatter(slots, 'ep', scatter_dimension=0, tiled=True)]
    pallas_call x0 -> x2, Pallas kernels: none -> 201 us  [the longest x1 125 us: project_and_return(): pl.pallas_call(return_kernel, name='return_rows', out_shape=jax.ShapeDtyp...]
    all_gather x1 -> x0, waiting for transfers between devices: 64.5 us -> none  [local_step(): all_rows = lax.all_gather(h_two, 'ep', axis=0, tiled=True)]
    dot_general x2 -> x0, matrix products: 38 us -> none  [the longest x1 24.3 us: expert_mlp(): jnp.einsum('emf,efd->emd', z_val, w_down, preferred_element_type=jnp.floa...]
    select_n x1 -> x0, other arithmetic: 15.9 us -> none  [local_step(): slots = jnp.where(mine, expert_out[:, None, :], jnp.zeros((), jnp.bfloat16))]
    all_gather x1 -> x0, blocking collectives: 14.5 us -> none  [local_step(): lax.all_gather(jnp.stack([expert_one, expert_two], axis=1), 'ep', axis=0,...]
    unnamed x43 -> x46, local copies, waits for them, and re-layouts: 2.52 us -> 16.1 us
  transfers between devices with their start and end apart: 2 -> 0, of which waited for: 2 -> 0; matrix products, arithmetic and copies ran while one was open for 0% -> 0% of each run, Pallas kernels for 0% -> 0%
where the time goes in v2:
time: 305 us; the launch traced here: 304 us
  Pallas kernels  201 us (66%)
  matrix products  55.5 us (18%)
  local copies, waits for them, and re-layouts  26.6 us (9%)
  other arithmetic  19.6 us (6%)
    pallas_call x1, Pallas kernels, project_and_return(): pl.pallas_call(return_kernel, name='return_rows', out_shape=jax.ShapeDtyp...  125 us
    pallas_call x1, Pallas kernels, gather_and_activate(): pl.pallas_call(functools.partial(gather_kernel, bounds), name='gather_row...  75.9 us
    unnamed x46, local copies, waits for them, and re-layouts  16.1 us
    dot_general x1, matrix products, attention_block(): jnp.einsum('tkgs,tskd->tkgd', p_cache, v_cache, preferred_element_type=jn...  15.7 us
    dot_general x1, matrix products, attention_block(): jnp.einsum('tkgd,tskd->tkgs', q_grp, k_cache, preferred_element_type=jnp....  15.4 us
    dot_general x1, matrix products, attention_block(): jnp.dot(attn_flat, w_out, preferred_element_type=jnp.float32)  8.42 us
    dot_general x1, matrix products, attention_block(): jnp.dot(h_one, w_query, preferred_element_type=jnp.float32)  8.17 us

profile of v2, /device:TPU:0, one launch (start us, length us, event | category | flops | bytes accessed | tf_op | source)
XLA Modules:
  0.0 303.5 jit_solution(9020347327036500101)
XLA Ops:
  0.7 1.5 convert_reduce_fusion
  2.2 1.7 fusion.11
  4.0 8.2 %convolution_add_fusion.1 = f32[128,2048]{1,0:T(8,128)S(1)} fusion(bf16[4096,2048]{1,0:T(8,128)(2,1)} %param.32, f32[2048]{0:T(1024)S(1)} %convert_element_type.83, bf16[128,4096]{1,0:T(8,128)(2,1)S(1)} %copy-done.2, f32[4096]{0:T(1024)S(1)} %convert_element_type.81, f32[4096]{0:T(1024)S(1)} %convert_element_type.80, f32[128]{0:T(128)S(1)} %add_rsqrt_fusion.1, ...), kind=kOutput, calls=%fused_computation.15 | convolution fusion | flops 2150891520 | bytes 18916352 | tf_op jit(solution)/shard_map/dot_general | solution.py:42
  12.4 1.7 slice_negate_fusion
  15.2 2.4 fusion.30
  17.6 3.1 %convolution_add_fusion.3 = f32[128,512]{1,0:T(8,128)S(1)} fusion(bf16[4096,512]{1,0:T(8,128)(2,1)} %param.34, f32[512]{0:T(512)S(1)} %convert_element_type.86, bf16[128,4096]{1,0:T(8,128)(2,1)S(1)} %copy-done.2, f32[4096]{0:T(1024)S(1)} %convert_element_type.81, f32[4096]{0:T(1024)S(1)} %convert_element_type.80, f32[128]{0:T(128)S(1)} %add_rsqrt_fusion.1, ...), kind=kOutput, calls=%fused_computation.33 | convolution fusion | flops 540082176 | bytes 5540864 | tf_op jit(solution)/shard_map/dot_general | solution.py:45
  22.9 15.4 %fusion.19 = (f32[128,4,4]{2,1,0:T(4,128)S(1)}, f32[128,4,4,256]{3,2,1,0:T(4,128)S(1)}) fusion(pred[128,256]{1,0:T(8,128)(4,1)S(1)} %iota_compare_fusion.1, bf16[128,4,4,128]{3,2,1,0:T(4,128)(2,1)} %copy-done.3, bf16[128,256,4,128]{3,2,1,0:T(4,128)(2,1)} %param.24), kind=kOutput, calls=%fused_computation.29 | convolution fusion | flops 135788544 | bytes 36216832 | tf_op jit(solution)/shard_map/tkgd,tskd->tkgs/dot_general | solution.py:50
  39.9 3.2 %fusion.27 = f32[128,4,4]{2,1,0:T(4,128)} fusion(f32[128,4,4,256]{3,2,1,0:T(4,128)S(1)} %get-tuple-element.22, f32[128,4,4]{2,1,0:T(4,128)S(1)} %copy.51, pred[128,256]{1,0:T(8,128)(4,1)} %copy-done.5), kind=kLoop, calls=%fused_computation.35 | loop fusion | flops 2095104 | bytes 2146304 | tf_op jit(solution)/shard_map/reduce_sum | solution.py:57
  43.1 1.7 copy.52
  44.8 1.3 fusion.49
  46.1 1.5 copy.53
  47.6 1.5 copy.55
  49.9 3.7 %fusion.26 = bf16[128,512]{1,0:T(8,128)(2,1)} fusion(bf16[4096,512]{1,0:T(8,128)(2,1)} %param.36, f32[512]{0:T(512)S(1)} %convert_element_type.91, bf16[128,4096]{1,0:T(8,128)(2,1)S(1)} %copy-done.2, f32[4096]{0:T(1024)} %copy-done.7, f32[4096]{0:T(1024)} %copy-done.6, f32[128]{0:T(128)} %copy-done.20, f32[128]{0:T(128)} %copy-done.18), kind=kOutput, calls=%fused_computation.34 | convolution fusion | flops 540147712 | bytes 5409792 | tf_op jit(solution)/shard_map/dot_general | solution.py:47
  53.5 1.6 reshape.150
  55.1 1.6 convert_element_type.93
  56.8 15.7 %fusion.23 = bf16[128,4,4,128]{3,2,1,0:T(4,128)(2,1)} fusion(bf16[128,256,4,128]{3,2,1,0:T(4,128)(2,1)} %param.25, f32[128,4,4,256]{3,2,1,0:T(4,128)S(1)} %get-tuple-element.22, f32[128,4,4]{2,1,0:T(4,128)} %copy.53, f32[128,4,4]{2,1,0:T(4,128)S(1)} %copy.51, pred[128,256]{1,0:T(8,128)(4,1)} %copy-done.5, f32[128,4,128]{2,1,0:T(4,128)} %convert_element_type.93, ...), kind=kOutput, calls=%fused_computation.31 | convolution fusion | flops 137625600 | bytes 36495360 | tf_op jit(solution)/shard_map/tkgs,tskd->tkgd/dot_general | solution.py:60
  72.4 1.4 reshape.151
  73.9 8.4 %convert_reduce_fusion.1 = (f32[128]{0:T(128)S(1)}, bf16[128,4096]{1,0:T(8,128)(2,1)S(1)}) fusion(f32[4096]{0:T(1024)S(1)} %convert_element_type.95, bf16[128,2048]{1,0:T(8,128)(2,1)S(1)} %reshape.151, bf16[2048,4096]{1,0:T(8,128)(2,1)} %param.38, bf16[128,4096]{1,0:T(8,128)(2,1)S(1)} %copy-done.2), kind=kOutput, calls=%fused_computation.10 | convolution fusion | flops 2150629376 | bytes 19415552 | tf_op jit(solution)/shard_map/dot_general | solution.py:63
  85.9 6.4 %copy.57 = bf16[1,4096,448]{2,1,0:T(8,128)(2,1)} copy(bf16[1,4096,448]{1,2,0:T(8,128)(2,1)} %param.43) | data formatting | bytes 7340032 | tf_op args[20]
  92.3 6.5 %copy.58 = bf16[1,4096,448]{2,1,0:T(8,128)(2,1)} copy(bf16[1,4096,448]{1,2,0:T(8,128)(2,1)} %param.44) | data formatting | bytes 7340032 | tf_op args[21]
  98.8 75.9 %gather_rows.1 = (bf16[8,256,448]{2,1,0:T(8,128)(2,1)}, bf16[8,256,128]{2,1,0:T(8,128)(2,1)}) custom-call(bf16[128,4224]{1,0:T(8,128)(2,1)} %fusion.28.h_ref, bf16[4096,448]{1,0:T(8,128)(2,1)} %bitcast.39, bf16[4096,448]{1,0:T(8,128)(2,1)} %bitcast.40), custom_call_target="tpu_custom_call" | custom-call | tf_op jit(solution)/shard_map/gather_rows/pallas_call | solution.py:323
  174.7 1.9 convert_xor_fusion.rel_ref
  176.6 124.7 %return_rows.1 = bf16[128,4096]{1,0:T(8,128)(2,1)} custom-call(bf16[8,256,448]{2,1,0:T(8,128)(2,1)} %get-tuple-element.5.z_ref, bf16[448,4096]{1,0:T(8,128)(2,1)} %bitcast.45, s32[8,128,128]{2,1,0:T(8,128)} %convert_xor_fusion.rel_ref, f32[128,128]{1,0:T(8,128)} %pad.9.gate_ref, bf16[128,4096]{1,0:T(8,128)(2,1)} %copy-done.1), custom_call_target="tpu_custom_call" | custom-call | tf_op jit(solution)/shard_map/return_rows/pallas_call | solution.py:341
  301.2 2.3 copy.76
  (82 shorter events, 9.2 us)
Async XLA Ops:
  0.6 82.7 %copy-start = (bf16[4096,16]{0,1:T(8,128)(2,1)S(1)}, bf16[4096,16]{0,1:T(8,128)(2,1)}, u32[]{:S(2)}) copy-start(bf16[4096,16]{0,1:T(8,128)(2,1)} %param.42) | copy-start | bytes 393220
  0.6 3.4 %copy-start.2 = (bf16[128,4096]{1,0:T(8,128)(2,1)S(1)}, bf16[128,4096]{1,0:T(8,128)(2,1)}, u32[]{:S(2)}) copy-start(bf16[128,4096]{1,0:T(8,128)(2,1)} %param.23) | copy-start | bytes 3145732
  0.7 3.3 %copy-start.9 = (bf16[4096]{0:T(1024)(128)(2,1)S(1)}, bf16[4096]{0:T(1024)(128)(2,1)}, u32[]{:S(2)}) copy-start(bf16[4096]{0:T(1024)(128)(2,1)} %param.30) | copy-start | bytes 24580
  0.7 3.3 %copy-start.10 = (bf16[4096]{0:T(1024)(128)(2,1)S(1)}, bf16[4096]{0:T(1024)(128)(2,1)}, u32[]{:S(2)}) copy-start(bf16[4096]{0:T(1024)(128)(2,1)} %param.31) | copy-start | bytes 24580
  0.7 3.3 %copy-start.15 = (bf16[2048]{0:T(1024)(128)(2,1)S(1)}, bf16[2048]{0:T(1024)(128)(2,1)}, u32[]{:S(2)}) copy-start(bf16[2048]{0:T(1024)(128)(2,1)} %param.33) | copy-start | bytes 12292
  2.2 15.4 %copy-start.18 = (f32[128]{0:T(128)}, f32[128]{0:T(128)S(1)}, u32[]{:S(2)}) copy-start(f32[128]{0:T(128)S(1)} %broadcast_multiply_fusion.2) | copy-start | bytes 1540
  3.9 13.7 %copy-start.20 = (f32[128]{0:T(128)}, f32[128]{0:T(128)S(1)}, u32[]{:S(2)}) copy-start(f32[128]{0:T(128)S(1)} %add_rsqrt_fusion.1) | copy-start | bytes 1540
  3.9 13.7 %copy-start.6 = (f32[4096]{0:T(1024)}, f32[4096]{0:T(1024)S(1)}, u32[]{:S(2)}) copy-start(f32[4096]{0:T(1024)S(1)} %convert_element_type.80) | copy-start | bytes 49156
  4.0 13.7 %copy-start.7 = (f32[4096]{0:T(1024)}, f32[4096]{0:T(1024)S(1)}, u32[]{:S(2)}) copy-start(f32[4096]{0:T(1024)S(1)} %convert_element_type.81) | copy-start | bytes 49156
  14.0 0.7 copy-start.19
  14.8 2.8 copy-start.17
  17.6 3.7 %copy-start.3 = (bf16[128,4,4,128]{3,2,1,0:T(4,128)(2,1)}, bf16[128,4,4,128]{3,2,1,0:T(4,128)(2,1)S(1)}, u32[]{:S(2)}) copy-start(bf16[128,4,4,128]{3,2,1,0:T(4,128)(2,1)S(1)} %fusion.30) | copy-start | bytes 1572868
  21.3 0.7 copy-start.4
  22.9 15.5 %copy-start.5 = (pred[128,256]{1,0:T(8,128)(4,1)}, pred[128,256]{1,0:T(8,128)(4,1)S(1)}, u32[]{:S(2)}) copy-start(pred[128,256]{1,0:T(8,128)(4,1)S(1)} %iota_compare_fusion.1) | copy-start | bytes 98308
  56.8 17.1 %copy-start.11 = (bf16[4096]{0:T(1024)(128)(2,1)S(1)}, bf16[4096]{0:T(1024)(128)(2,1)}, u32[]{:S(2)}) copy-start(bf16[4096]{0:T(1024)(128)(2,1)} %param.39) | copy-start | bytes 24580
  73.9 8.9 %copy-start.12 = (bf16[4096]{0:T(1024)(128)(2,1)S(1)}, bf16[4096]{0:T(1024)(128)(2,1)}, u32[]{:S(2)}) copy-start(bf16[4096]{0:T(1024)(128)(2,1)} %param.40) | copy-start | bytes 24580
  73.9 9.0 %copy-start.13 = (bf16[4096]{0:T(1024)(128)(2,1)S(1)}, bf16[4096]{0:T(1024)(128)(2,1)}, u32[]{:S(2)}) copy-start(bf16[4096]{0:T(1024)(128)(2,1)} %param.41) | copy-start | bytes 24580
  82.3 1.4 copy-start.1
  82.3 1.0 copy-start.8
  82.4 1.4 copy-start.14
  82.4 1.5 copy-start.16

commit v3 on v2

--- a/solution.py
+++ b/solution.py
@@ -10,78 +10,236 @@
 ROPE_BASE = 10000.0
 LN_EPS = 1e-5
 
-
-def layer_norm(values_in, gain, bias):
-    mean_val = jnp.mean(values_in, axis=-1, keepdims=True)
-    centered = values_in - mean_val
-    var_val = jnp.mean(centered * centered, axis=-1, keepdims=True)
-    return centered * lax.rsqrt(var_val + LN_EPS) * gain.astype(jnp.float32) + bias.astype(jnp.float32)
-
-
-def rope_tables(positions, head_dim):
-    half_dim = head_dim // 2
-    inv_freq = ROPE_BASE ** (jnp.arange(half_dim, dtype=jnp.float32) * (-2.0 / head_dim))
-    angles = positions.astype(jnp.float32)[:, None] * inv_freq[None, :]
-    angles = jnp.concatenate([angles, angles], axis=-1)
-    return jnp.cos(angles), jnp.sin(angles)
-
-
-def apply_rope(values_in, cos_tab, sin_tab):
-    half_dim = values_in.shape[-1] // 2
-    rotated = jnp.concatenate([-values_in[..., half_dim:], values_in[..., :half_dim]], axis=-1)
-    return values_in * cos_tab[:, None, :] + rotated * sin_tab[:, None, :]
-
-
-def attention_block(tokens, k_cache, v_cache, positions, ln1_gain, ln1_bias, w_query, b_query, w_key, b_key, w_value, b_value, w_out, b_out):
-    tok_count, seq_len, kv_heads, head_dim = k_cache.shape
-    num_heads = w_query.shape[1] // head_dim
-    group_size = num_heads // kv_heads
-    x_f = tokens.astype(jnp.float32)
-    h_one = layer_norm(x_f, ln1_gain, ln1_bias).astype(jnp.bfloat16)
-    cos_tab, sin_tab = rope_tables(positions, head_dim)
-    q_lin = jnp.dot(h_one, w_query, preferred_element_type=jnp.float32) + b_query.astype(jnp.float32)
-    q_rot = apply_rope(q_lin.reshape(tok_count, num_heads, head_dim), cos_tab, sin_tab).astype(jnp.bfloat16)
-    q_grp = q_rot.reshape(tok_count, kv_heads, group_size, head_dim)
-    k_lin = jnp.dot(h_one, w_key, preferred_element_type=jnp.float32) + b_key.astype(jnp.float32)
-    key_new = apply_rope(k_lin.reshape(tok_count, kv_heads, head_dim), cos_tab, sin_tab).astype(jnp.bfloat16)
-    v_lin = jnp.dot(h_one, w_value, preferred_element_type=jnp.float32) + b_value.astype(jnp.float32)
-    value_new = v_lin.astype(jnp.bfloat16).reshape(tok_count, kv_heads, head_dim)
-    score_scale = head_dim ** -0.5
-    s_cache = jnp.einsum('tkgd,tskd->tkgs', q_grp, k_cache, preferred_element_type=jnp.float32) * score_scale
-    valid_mask = jnp.arange(seq_len)[None, None, None, :] < positions[:, None, None, None]
-    s_cache = jnp.where(valid_mask, s_cache, -jnp.inf)
-    s_new = jnp.einsum('tkgd,tkd->tkg', q_grp, key_new, preferred_element_type=jnp.float32) * score_scale
-    top_val = jnp.maximum(jnp.max(s_cache, axis=-1), s_new)
-    e_cache = jnp.exp(s_cache - top_val[..., None])
-    e_new = jnp.exp(s_new - top_val)
-    denom_sum = jnp.sum(e_cache, axis=-1) + e_new
-    p_cache = (e_cache / denom_sum[..., None]).astype(jnp.bfloat16)
-    p_new = (e_new / denom_sum).astype(jnp.bfloat16)
-    attn_vals = jnp.einsum('tkgs,tskd->tkgd', p_cache, v_cache, preferred_element_type=jnp.float32)
-    attn_vals = attn_vals + p_new.astype(jnp.float32)[..., None] * value_new.astype(jnp.float32)[:, :, None, :]
-    attn_flat = attn_vals.astype(jnp.bfloat16).reshape(tok_count, num_heads * head_dim)
-    x_mid = (x_f + jnp.dot(attn_flat, w_out, preferred_element_type=jnp.float32) + b_out.astype(jnp.float32)).astype(jnp.bfloat16)
-    return x_mid, key_new, value_new
-
-
-def router_gates(h_two, w_router, expert_one, expert_two, eligible):
-    logits = jnp.dot(h_two, w_router, preferred_element_type=jnp.float32)
-    expert_ids = jnp.arange(logits.shape[1])[None, :]
-    hit_one = expert_ids == expert_one[:, None]
-    hit_two = expert_ids == expert_two[:, None]
-    keep_one = eligible == 1
-    keep_two = keep_one & jnp.logical_not(hit_one)
-    prob_one = jax.nn.softmax(jnp.where(keep_one, logits, -jnp.inf), axis=-1)
-    prob_two = jax.nn.softmax(jnp.where(keep_two, logits, -jnp.inf), axis=-1)
-    gate_one = jnp.sum(jnp.where(hit_one, prob_one, 0.0), axis=-1)
-    gate_two = jnp.sum(jnp.where(hit_two, prob_two, 0.0), axis=-1)
-    return gate_one, gate_two
-
-
 MESH = pl.DeviceIdType.MESH
 ORDERS = ((1, 2, 4), (2, 4, 1), (4, 1, 2))
 LANES = 128
 WIDTH = 256
+ALONG = (((1,), (1,)), ((), ()))
+
+
+TILE = 256
+GROUP = 8
+DEPTH = 3
+CHUNK = 64
+
+
+def normed(x_f, gain_ref, bias_ref):
+    mean_val = jnp.mean(x_f, axis=-1, keepdims=True)
+    centered = x_f - mean_val
+    var_val = jnp.mean(centered * centered, axis=-1, keepdims=True)
+    return centered * lax.rsqrt(var_val + LN_EPS) * gain_ref[...].astype(jnp.float32) + bias_ref[...].astype(jnp.float32)
+
+
+def qkv_kernel(q_steps, kv_steps, x_ref, gain_ref, bias_ref, wq_ref, wk_ref, wv_ref, bq_ref, bk_ref, bv_ref, cos_ref, sin_ref, q_ref, k_ref, v_ref, h_ref):
+    step = pl.program_id(0)
+
+    @pl.when(step == 0)
+    def _():
+        h_ref[...] = normed(x_ref[...].astype(jnp.float32), gain_ref, bias_ref).astype(jnp.bfloat16)
+
+    def turned(w_ref, b_ref, o_ref):
+        lin = jnp.dot(h_ref[...], w_ref[...], preferred_element_type=jnp.float32) + b_ref[...].astype(jnp.float32)
+        for lo in range(0, TILE, LANES):
+            head = lin[:, lo:lo + LANES]
+            o_ref[:, lo:lo + LANES] = (head * cos_ref[...] + pltpu.roll(head, LANES // 2, 1) * sin_ref[...]).astype(jnp.bfloat16)
+
+    @pl.when(step < q_steps)
+    def _():
+        turned(wq_ref, bq_ref, q_ref)
+
+    @pl.when((step >= q_steps) & (step < q_steps + kv_steps))
+    def _():
+        turned(wk_ref, bk_ref, k_ref)
+
+    @pl.when(step >= q_steps + kv_steps)
+    def _():
+        lin = jnp.dot(h_ref[...], wv_ref[...], preferred_element_type=jnp.float32)
+        v_ref[...] = (lin + bv_ref[...].astype(jnp.float32)).astype(jnp.bfloat16)
+
+
+def project_qkv(tokens, gain, bias, w_query, b_query, w_key, b_key, w_value, b_value, positions):
+    rows, d_model = tokens.shape
+    q_dim, kv_dim = w_query.shape[1], w_key.shape[1]
+    q_steps, kv_steps = q_dim // TILE, kv_dim // TILE
+    half_dim = LANES // 2
+    inv_freq = ROPE_BASE ** (jnp.arange(half_dim, dtype=jnp.float32) * (-2.0 / LANES))
+    angles = positions.astype(jnp.float32)[:, None] * inv_freq[None, :]
+    cos_half, sin_half = jnp.cos(angles), jnp.sin(angles)
+    cos_tab = jnp.concatenate([cos_half, cos_half], axis=-1)
+    sin_tab = jnp.concatenate([-sin_half, sin_half], axis=-1)
+
+    def at_q(i):
+        return 0, jnp.minimum(i, q_steps - 1)
+
+    def at_k(i):
+        return 0, jnp.clip(i - q_steps, 0, kv_steps - 1)
+
+    def at_v(i):
+        return 0, jnp.clip(i - q_steps - kv_steps, 0, kv_steps - 1)
+
+    def whole(shape):
+        return pl.BlockSpec(shape, lambda i: (0, 0))
+
+    return pl.pallas_call(
+        functools.partial(qkv_kernel, q_steps, kv_steps),
+        name='project_qkv',
+        grid=(q_steps + 2 * kv_steps,),
+        out_shape=(jax.ShapeDtypeStruct((rows, q_dim), jnp.bfloat16), jax.ShapeDtypeStruct((rows, kv_dim), jnp.bfloat16), jax.ShapeDtypeStruct((rows, kv_dim), jnp.bfloat16)),
+        in_specs=[whole((rows, d_model)), whole((1, d_model)), whole((1, d_model)),
+                  pl.BlockSpec((d_model, TILE), at_q), pl.BlockSpec((d_model, TILE), at_k), pl.BlockSpec((d_model, TILE), at_v),
+                  pl.BlockSpec((1, TILE), at_q), pl.BlockSpec((1, TILE), at_k), pl.BlockSpec((1, TILE), at_v),
+                  whole((rows, LANES)), whole((rows, LANES))],
+        out_specs=(pl.BlockSpec((rows, TILE), at_q), pl.BlockSpec((rows, TILE), at_k), pl.BlockSpec((rows, TILE), at_v)),
+        scratch_shapes=[pltpu.VMEM((rows, d_model), jnp.bfloat16)],
+    )(tokens, gain[None], bias[None], w_query, w_key, w_value, b_query[None], b_key[None], b_value[None], cos_tab, sin_tab)
+
+
+def attend_kernel(order_ref, pos_ref, span_ref, q_ref, kn_ref, vn_ref, k_hbm, v_hbm, o_ref, k_buf, v_buf, where_ref, sems):
+    groups = order_ref.shape[0] // GROUP
+    heads = q_ref.shape[1]
+    kv_heads = k_hbm.shape[1] // (k_hbm.shape[1] // 4)
+    spans = k_hbm.shape[1] // (CHUNK * kv_heads)
+    scale = LANES ** -0.5
+    col = lax.broadcasted_iota(jnp.int32, where_ref.shape, 1)
+    row = lax.broadcasted_iota(jnp.int32, where_ref.shape, 0)
+    where_ref[...] = jnp.where(col % kv_heads == row // (heads // kv_heads), col // kv_heads, 1 << 20)
+
+    def copies(g, n):
+        slot = lax.rem(g, DEPTH)
+        size = n * CHUNK * kv_heads
+        for j in range(GROUP):
+            t = order_ref[g * GROUP + j]
+            yield pltpu.make_async_copy(k_hbm.at[t, pl.ds(0, size)], k_buf.at[slot, j, pl.ds(0, size)], sems.at[slot, 0])
+            yield pltpu.make_async_copy(v_hbm.at[t, pl.ds(0, size)], v_buf.at[slot, j, pl.ds(0, size)], sems.at[slot, 1])
+
+    def each_span(g, body):
+        for n in range(1, spans + 1):
+            @pl.when(span_ref[g] == n)
+            def _(n=n):
+                body(n)
+
+    def fetch(g):
+        def body(n):
+            for copy in copies(g, n):
+                copy.start()
+        each_span(g, body)
+
+    for g in range(DEPTH - 1):
+        fetch(jnp.int32(g))
+
+    @pl.loop(0, groups)
+    def _(g):
+        @pl.when(g + DEPTH - 1 < groups)
+        def _():
+            fetch(g + DEPTH - 1)
+
+        slot = lax.rem(g, DEPTH)
+
+        def body(n):
+            size = n * CHUNK * kv_heads
+            for copy in copies(g, n):
+                copy.wait()
+            for j in range(GROUP):
+                t = order_ref[g * GROUP + j]
+                pos = pos_ref[g * GROUP + j]
+                q_val = q_ref[t]
+                s_val = lax.dot_general(q_val, k_buf[slot, j, :size], (((1,), (1,)), ((), ())), preferred_element_type=jnp.float32) * scale
+                s_new = jnp.sum(q_val.astype(jnp.float32) * kn_ref[t].astype(jnp.float32), axis=1, keepdims=True) * scale
+                s_val = jnp.where(where_ref[:, :size] < pos, s_val, -jnp.inf)
+                top = jnp.maximum(jnp.max(s_val, axis=1, keepdims=True), s_new)
+                e_val, e_new = jnp.exp(s_val - top), jnp.exp(s_new - top)
+                inv = 1.0 / (jnp.sum(e_val, axis=1, keepdims=True) + e_new)
+                p_val = (e_val * inv).astype(jnp.bfloat16)
+                p_new = (e_new * inv).astype(jnp.bfloat16).astype(jnp.float32)
+                a_val = jnp.dot(p_val, v_buf[slot, j, :size], preferred_element_type=jnp.float32)
+                o_ref[t] = (a_val + p_new * vn_ref[t].astype(jnp.float32)).astype(jnp.bfloat16)
+        each_span(g, body)
+
+
+def attend(q_val, k_new, v_new, k_cache, v_cache, positions):
+    rows, seq_len, kv_heads, head_dim = k_cache.shape
+    heads = q_val.shape[1] // head_dim
+    ids = jnp.arange(rows, dtype=jnp.int32)
+    ahead = (positions[None, :] < positions[:, None]) | ((positions[None, :] == positions[:, None]) & (ids[None, :] < ids[:, None]))
+    rank = jnp.sum(ahead.astype(jnp.int32), axis=1)
+    hit = rank[None, :] == ids[:, None]
+    order = jnp.sum(jnp.where(hit, ids[None, :], 0), axis=1)
+    pos_sorted = jnp.sum(jnp.where(hit, positions[None, :], 0), axis=1)
+    span = jnp.clip((pos_sorted[GROUP - 1::GROUP] + CHUNK - 1) // CHUNK, 1, seq_len // CHUNK)
+
+    def spread(val):
+        return jnp.repeat(val.reshape(rows, kv_heads, head_dim), heads // kv_heads, axis=1)
+
+    vmem = pl.BlockSpec(memory_space=pltpu.VMEM)
+    smem = pl.BlockSpec(memory_space=pltpu.SMEM)
+    hbm = pl.BlockSpec(memory_space=pl.ANY)
+    flat = (rows, seq_len * kv_heads, head_dim)
+    return pl.pallas_call(
+        attend_kernel,
+        name='attend',
+        out_shape=jax.ShapeDtypeStruct((rows, heads, head_dim), jnp.bfloat16),
+        in_specs=[smem, smem, smem, vmem, vmem, vmem, hbm, hbm],
+        out_specs=vmem,
+        scratch_shapes=[
+            pltpu.VMEM((DEPTH, GROUP) + flat[1:], jnp.bfloat16), pltpu.VMEM((DEPTH, GROUP) + flat[1:], jnp.bfloat16),
+            pltpu.VMEM((heads, flat[1]), jnp.int32),
+            pltpu.SemaphoreType.DMA((DEPTH, 2))],
+        compiler_params=pltpu.CompilerParams(vmem_limit_bytes=48 * 1024 * 1024),
+    )(order, pos_sorted, span, q_val.reshape(rows, heads, head_dim), spread(k_new), spread(v_new), k_cache.reshape(flat), v_cache.reshape(flat))
+
+
+def mix_kernel(a_ref, w_ref, x_ref, b_ref, gain_ref, bias_ref, wr_ref, pick_ref, elig_ref, ids_ref, x_out, h_out, gate_out, x_all):
+    step = pl.program_id(0)
+    width = w_ref.shape[1]
+    d_model = x_all.shape[1]
+    acc = jnp.dot(a_ref[...], w_ref[...], preferred_element_type=jnp.float32)
+    x_mid = (x_ref[...].astype(jnp.float32) + acc + b_ref[...].astype(jnp.float32)).astype(jnp.bfloat16)
+    x_out[...] = x_mid
+    x_all[:, pl.ds(pl.multiple_of(step * width, width), width)] = x_mid
+
+    @pl.when(step == pl.num_programs(0) - 1)
+    def _():
+        h_two = normed(x_all[...].astype(jnp.float32), gain_ref, bias_ref).astype(jnp.bfloat16)
+        h_out[:, :d_model] = h_two
+        h_out[:, d_model:] = ids_ref[...]
+        logits = lax.dot_general(h_two, wr_ref[...], (((1,), (1,)), ((), ())), preferred_element_type=jnp.float32)
+        experts = lax.broadcasted_iota(jnp.int32, logits.shape, 1)
+        hit_one = experts == pick_ref[:, 0:1]
+        hit_two = experts == pick_ref[:, 1:2]
+        keep_one = elig_ref[...] == 1
+
+        def gate(keep, hit):
+            val = jnp.where(keep, logits, -jnp.inf)
+            e_val = jnp.exp(val - jnp.max(val, axis=1, keepdims=True))
+            return jnp.sum(jnp.where(hit, e_val, 0.0), axis=1, keepdims=True) / jnp.sum(e_val, axis=1, keepdims=True)
+
+        lane = lax.broadcasted_iota(jnp.int32, gate_out.shape, 1)
+        gate_out[...] = jnp.where(lane == 0, gate(keep_one, hit_one), gate(keep_one & jnp.logical_not(hit_one), hit_two))
+
+
+def mix(attn, w_out, tokens, b_out, gain, bias, w_router, expert_one, expert_two, eligible):
+    rows, d_model = tokens.shape
+    inner = w_out.shape[0]
+    width = 2 * TILE
+    picks = jnp.stack([expert_one, expert_two], axis=1)
+    ids = jnp.pad(picks.astype(jnp.bfloat16), ((0, 0), (0, LANES - 2)))
+
+    def whole(shape):
+        return pl.BlockSpec(shape, lambda i: (0, 0))
+
+    def tile(height):
+        return pl.BlockSpec((height, width), lambda i: (0, i))
+
+    return pl.pallas_call(
+        mix_kernel,
+        name='mix',
+        grid=(d_model // width,),
+        out_shape=(jax.ShapeDtypeStruct((rows, d_model), jnp.bfloat16), jax.ShapeDtypeStruct((rows, d_model + LANES), jnp.bfloat16), jax.ShapeDtypeStruct((rows, LANES), jnp.float32)),
+        in_specs=[whole((rows, inner)), tile(inner), tile(rows), tile(1), whole((1, d_model)), whole((1, d_model)),
+                  whole((w_router.shape[1], d_model)), whole((rows, 2)), whole(eligible.shape), whole((rows, LANES))],
+        out_specs=(tile(rows), whole((rows, d_model + LANES)), whole((rows, LANES))),
+        scratch_shapes=[pltpu.VMEM((rows, d_model), jnp.bfloat16)],
+    )(attn, w_out, tokens, b_out[None], gain[None], bias[None], w_router.T, picks, eligible, ids)
 
 
 def flip(me, bit):
@@ -126,10 +284,10 @@
         u_val = v_val = None
         for f in range(3):
             lo, hi = bounds[f]
-            hi = min(hi, wg_ref.shape[0])
+            hi = min(hi, wg_ref.shape[1])
             x_val = bufs[f][pair, :, : hi - lo]
-            u_part = jnp.dot(x_val, wg_ref[lo:hi, :], preferred_element_type=jnp.float32)
-            v_part = jnp.dot(x_val, wu_ref[lo:hi, :], preferred_element_type=jnp.float32)
+            u_part = lax.dot_general(x_val, wg_ref[:, lo:hi], ALONG, preferred_element_type=jnp.float32)
+            v_part = lax.dot_general(x_val, wu_ref[:, lo:hi], ALONG, preferred_element_type=jnp.float32)
             u_val = u_part if u_val is None else u_val + u_part
             v_val = v_part if v_val is None else v_val + v_part
         z_ref[pair] = (jax.nn.silu(u_val) * v_val).astype(jnp.bfloat16)
@@ -311,11 +469,9 @@
     sweep(drain)
 
 
-def gather_and_activate(h_two, expert_one, expert_two, w_gate, w_up):
-    rows, d_model = h_two.shape
-    d_ff = w_gate.shape[1]
-    ids = jnp.pad(jnp.stack([expert_one, expert_two], axis=1).astype(jnp.bfloat16), ((0, 0), (0, LANES - 2)))
-    h_ext = jnp.concatenate([h_two, ids], axis=1)
+def gather_and_activate(h_ext, w_gate, w_up):
+    rows, d_model = h_ext.shape[0], h_ext.shape[1] - LANES
+    d_ff = w_gate.shape[0]
     tiles = (d_model + LANES) // LANES
     cuts = [LANES * ((tiles * f + 2) // 3) for f in range(4)]
     bounds = tuple((cuts[f], cuts[f + 1]) for f in range(3))
@@ -360,13 +516,14 @@
 
 def solution(mesh):
     def local_step(tokens, k_cache, v_cache, positions, expert_one, expert_two, eligible, ln1_gain, ln1_bias, w_query, b_query, w_key, b_key, w_value, b_value, w_out, b_out, ln2_gain, ln2_bias, w_router, w_gate, w_up, w_down):
-        x_mid, key_new, value_new = attention_block(tokens, k_cache, v_cache, positions, ln1_gain, ln1_bias, w_query, b_query, w_key, b_key, w_value, b_value, w_out, b_out)
-        h_two = layer_norm(x_mid.astype(jnp.float32), ln2_gain, ln2_bias).astype(jnp.bfloat16)
-        gate_one, gate_two = router_gates(h_two, w_router, expert_one, expert_two, eligible)
-        z_val, ids = gather_and_activate(h_two, expert_one, expert_two, w_gate[0], w_up[0])
-        rel = ids[:, :h_two.shape[0]].astype(jnp.int32) ^ lax.axis_index('ep')
-        gates = jnp.pad(jnp.stack([gate_one, gate_two], axis=1), ((0, 0), (0, LANES - 2)))
+        rows, seq_len, kv_heads, head_dim = k_cache.shape
+        q_val, k_val, v_val = project_qkv(tokens, ln1_gain, ln1_bias, w_query, b_query, w_key, b_key, w_value, b_value, positions)
+        attn = attend(q_val, k_val, v_val, k_cache, v_cache, positions).reshape(rows, -1)
+        x_mid, h_ext, gates = mix(attn, w_out, tokens, b_out, ln2_gain, ln2_bias, w_router, expert_one, expert_two, eligible)
+        z_val, ids = gather_and_activate(h_ext, w_gate[0].T, w_up[0].T)
+        rel = ids[:, :rows].astype(jnp.int32) ^ lax.axis_index('ep')
         tokens_out = project_and_return(z_val, w_down[0], rel, gates, x_mid)
+        key_new, value_new = k_val.reshape(rows, kv_heads, head_dim), v_val.reshape(rows, kv_heads, head_dim)
         return tokens_out, key_new, value_new
 
     row_spec = P('ep', None)

time: 305 us -> 303 us (level)
  Pallas kernels: 201 us -> 280 us
  matrix products: 55.5 us -> 0 us
  other arithmetic: 19.6 us -> 3.86 us
  local copies, waits for them, and re-layouts: 26.6 us -> 17.2 us
    pallas_call x0 -> x3, Pallas kernels: none -> 80 us  [the longest x1 50.4 us: attend(): pl.pallas_call(attend_kernel, name='attend', out_shape=jax.ShapeDtypeStru...]
    dot_general x8 -> x0, matrix products: 55.5 us -> none  [the longest x1 15.7 us: attention_block(): jnp.einsum('tkgs,tskd->tkgd', p_cache, v_cache, preferred_element_type=jn...]
    unnamed x46 -> x22, local copies, waits for them, and re-layouts: 16.1 us -> 5.13 us
    broadcast_in_dim x0 -> x10, local copies, waits for them, and re-layouts: none -> 8.59 us  [the longest x1 1.3 us: project_qkv(): gain[None]]
    reduce_sum x7 -> x2, other arithmetic: 6.92 us -> 0.29 us  [the longest x1 0.17 us: attend(): rank = jnp.sum(ahead.astype(jnp.int32), axis=1)]
    convert_element_type x14 -> x2, other arithmetic: 6.73 us -> 0.67 us  [the longest x1 0.66 us: project_qkv(): angles = positions.astype(jnp.float32)[:, None] * inv_freq[None, :]]
where the time goes in v3:
time: 303 us; the launch traced here: 302 us
  Pallas kernels  280 us (92%)
  local copies, waits for them, and re-layouts  17.2 us (6%)
  other arithmetic  3.86 us (1%)
    pallas_call x1, Pallas kernels, project_and_return(): pl.pallas_call(return_kernel, name='return_rows', out_shape=jax.ShapeDtyp...  122 us
    pallas_call x1, Pallas kernels, gather_and_activate(): pl.pallas_call(functools.partial(gather_kernel, bounds), name='gather_row...  77.3 us
    pallas_call x1, Pallas kernels, attend(): pl.pallas_call(attend_kernel, name='attend', out_shape=jax.ShapeDtypeStru...  50.4 us
    pallas_call x1, Pallas kernels, project_qkv(): pl.pallas_call(functools.partial(qkv_kernel, q_steps, kv_steps), name='pr...  17.4 us
    pallas_call x1, Pallas kernels, mix(): pl.pallas_call(mix_kernel, name='mix', grid=(d_model // width,), out_shap...  12.2 us

profile of v3, /device:TPU:0, one launch (start us, length us, event | category | flops | bytes accessed | tf_op | source)
XLA Modules:
  0.0 301.6 jit_solution(15972971432212472658)
XLA Ops:
  0.6 0.7 convert_element_type.15
  1.6 0.7 pad_maximum_fusion
  2.4 1.3 broadcast_in_dim.57.gain_ref
  3.7 1.3 broadcast_in_dim.58.bias_ref
  5.0 1.3 broadcast_in_dim.59.bq_ref
  6.3 1.3 broadcast_in_dim.60.bk_ref
  7.5 1.3 broadcast_in_dim.61.bv_ref
  8.8 17.4 %project_qkv.1 = (bf16[128,2048]{1,0:T(8,128)(2,1)}, bf16[128,512]{1,0:T(8,128)(2,1)}, bf16[128,512]{1,0:T(8,128)(2,1)}) custom-call(bf16[128,4096]{1,0:T(8,128)(2,1)} %x_ref.3, bf16[1,4096]{1,0:T(2,128)(2,1)} %broadcast_in_dim.57.gain_ref, bf16[1,4096]{1,0:T(2,128)(2,1)} %broadcast_in_dim.58.bias_ref, bf16[4096,2048]{1,0:T(8,128)(2,1)} %wq_ref.1, ...), custom_call_target="tpu_custom_call" | custom-call | tf_op jit(solution)/shard_map/project_qkv/pallas_call | solution.py:83
  26.2 0.9 reshape.42
  27.4 0.9 reshape.44
  28.5 1.1 copy.38
  30.2 50.4 %attend.1 = bf16[128,16,128]{2,1,0:T(8,128)(2,1)S(1)} custom-call(s32[128]{0:T(128)S(1)} %get-tuple-element.20.order_ref, s32[128]{0:T(128)S(1)} %get-tuple-element.19.pos_ref, s32[16]{0:T(128)S(1)} %fusion.3.span_ref, bf16[128,16,128]{2,1,0:T(8,128)(2,1)S(1)} %bitcast.22, bf16[128,16,128]{2,1,0:T(8,128)(2,1)S(1)} %bitcast.20, ...), custom_call_target="tpu_custom_call" | custom-call | tf_op jit(solution)/shard_map/attend/pallas_call | solution.py:177
  80.6 0.9 copy.41
  81.5 0.7 copy.36.pick_ref
  82.4 0.6 pad.4.ids_ref
  83.0 0.7 copy.37.elig_ref
  83.7 0.6 broadcast_in_dim.64.b_ref
  84.4 0.6 broadcast_in_dim.65.gain_ref
  85.0 0.6 broadcast_in_dim.66.bias_ref
  85.6 12.2 %mix.1 = (bf16[128,4096]{1,0:T(8,128)(2,1)}, bf16[128,4224]{1,0:T(8,128)(2,1)}, f32[128,128]{1,0:T(8,128)}) custom-call(bf16[128,2048]{1,0:T(8,128)(2,1)} %bitcast.29, bf16[2048,4096]{1,0:T(8,128)(2,1)} %w_ref.1, bf16[128,4096]{1,0:T(8,128)(2,1)} %x_ref.3, bf16[1,4096]{1,0:T(2,128)(2,1)} %broadcast_in_dim.64.b_ref, ...), custom_call_target="tpu_custom_call" | custom-call | tf_op jit(solution)/shard_map/mix/pallas_call | solution.py:233
  97.8 77.3 %gather_rows.1 = (bf16[8,256,448]{2,1,0:T(8,128)(2,1)}, bf16[8,256,128]{2,1,0:T(8,128)(2,1)}) custom-call(bf16[128,4224]{1,0:T(8,128)(2,1)} %get-tuple-element.14.h_ref, bf16[448,4096]{1,0:T(8,128)(2,1)} %bitcast.26, bf16[448,4096]{1,0:T(8,128)(2,1)} %bitcast.27), custom_call_target="tpu_custom_call" | custom-call | tf_op jit(solution)/shard_map/gather_rows/pallas_call | solution.py:479
  175.1 1.8 convert_xor_fusion.rel_ref
  176.9 122.4 %return_rows.1 = bf16[128,4096]{1,0:T(8,128)(2,1)} custom-call(bf16[8,256,448]{2,1,0:T(8,128)(2,1)} %get-tuple-element.15.z_ref, bf16[448,4096]{1,0:T(8,128)(2,1)} %bitcast.28, s32[8,128,128]{2,1,0:T(8,128)} %convert_xor_fusion.rel_ref, f32[128,128]{1,0:T(8,128)} %get-tuple-element.17.gate_ref, bf16[128,4096]{1,0:T(8,128)(2,1)} %get-tuple-element.18.x_ref), custom_call_target="tpu_custom_call" | custom-call | tf_op jit(solution)/shard_map/return_rows/pallas_call | solution.py:497
  299.3 2.3 copy.43
  (28 shorter events, 1.3 us)
Async XLA Ops:
  8.8 20.9 %copy-start.8 = (s32[128]{0:T(128)S(1)}, s32[128]{0:T(128)}, u32[]{:S(2)}) copy-start(s32[128]{0:T(128)} %param.26) | copy-start | bytes 1540
  27.2 53.4 %copy-start = (bf16[128,4,128]{2,1,0:T(4,128)(2,1)}, bf16[128,4,128]{2,1,0:T(4,128)(2,1)S(1)}, u32[]{:S(2)}) copy-start(bf16[128,4,128]{2,1,0:T(4,128)(2,1)S(1)} %reshape.42) | copy-start | bytes 393220
  28.3 52.3 %copy-start.1 = (bf16[128,4,128]{2,1,0:T(4,128)(2,1)}, bf16[128,4,128]{2,1,0:T(4,128)(2,1)S(1)}, u32[]{:S(2)}) copy-start(bf16[128,4,128]{2,1,0:T(4,128)(2,1)S(1)} %reshape.44) | copy-start | bytes 393220
  30.1 51.4 %copy-start.6 = (s32[128]{0:T(128)S(1)}, s32[128]{0:T(128)}, u32[]{:S(2)}) copy-start(s32[128]{0:T(128)} %param.28) | copy-start | bytes 1540
  30.1 51.4 %copy-start.7 = (s32[128]{0:T(128)S(1)}, s32[128]{0:T(128)}, u32[]{:S(2)}) copy-start(s32[128]{0:T(128)} %param.27) | copy-start | bytes 1540
  30.1 52.9 %copy-start.2 = (s32[128,16]{0,1:T(8,128)S(1)}, s32[128,16]{0,1:T(8,128)}, u32[]{:S(2)}) copy-start(s32[128,16]{0,1:T(8,128)} %param.29) | copy-start | bytes 24580
  30.1 53.6 %copy-start.3 = (bf16[4096]{0:T(1024)(128)(2,1)S(1)}, bf16[4096]{0:T(1024)(128)(2,1)}, u32[]{:S(2)}) copy-start(bf16[4096]{0:T(1024)(128)(2,1)} %param.39) | copy-start | bytes 24580
  30.1 54.2 %copy-start.4 = (bf16[4096]{0:T(1024)(128)(2,1)S(1)}, bf16[4096]{0:T(1024)(128)(2,1)}, u32[]{:S(2)}) copy-start(bf16[4096]{0:T(1024)(128)(2,1)} %param.40) | copy-start | bytes 24580
  30.2 54.8 %copy-start.5 = (bf16[4096]{0:T(1024)(128)(2,1)S(1)}, bf16[4096]{0:T(1024)(128)(2,1)}, u32[]{:S(2)}) copy-start(bf16[4096]{0:T(1024)(128)(2,1)} %param.41) | copy-start | bytes 24580

commit v4 on v3

--- a/solution.py
+++ b/solution.py
@@ -17,100 +17,46 @@
 ALONG = (((1,), (1,)), ((), ()))
 
 
-TILE = 256
+TILE = 512
+HALF = 2048
 GROUP = 8
+PART = 4
 DEPTH = 3
 CHUNK = 64
 
 
-def normed(x_f, gain_ref, bias_ref):
+def normed(x_f, gain, bias):
     mean_val = jnp.mean(x_f, axis=-1, keepdims=True)
     centered = x_f - mean_val
     var_val = jnp.mean(centered * centered, axis=-1, keepdims=True)
-    return centered * lax.rsqrt(var_val + LN_EPS) * gain_ref[...].astype(jnp.float32) + bias_ref[...].astype(jnp.float32)
-
-
-def qkv_kernel(q_steps, kv_steps, x_ref, gain_ref, bias_ref, wq_ref, wk_ref, wv_ref, bq_ref, bk_ref, bv_ref, cos_ref, sin_ref, q_ref, k_ref, v_ref, h_ref):
-    step = pl.program_id(0)
-
-    @pl.when(step == 0)
-    def _():
-        h_ref[...] = normed(x_ref[...].astype(jnp.float32), gain_ref, bias_ref).astype(jnp.bfloat16)
-
-    def turned(w_ref, b_ref, o_ref):
-        lin = jnp.dot(h_ref[...], w_ref[...], preferred_element_type=jnp.float32) + b_ref[...].astype(jnp.float32)
-        for lo in range(0, TILE, LANES):
-            head = lin[:, lo:lo + LANES]
-            o_ref[:, lo:lo + LANES] = (head * cos_ref[...] + pltpu.roll(head, LANES // 2, 1) * sin_ref[...]).astype(jnp.bfloat16)
-
-    @pl.when(step < q_steps)
-    def _():
-        turned(wq_ref, bq_ref, q_ref)
-
-    @pl.when((step >= q_steps) & (step < q_steps + kv_steps))
-    def _():
-        turned(wk_ref, bk_ref, k_ref)
-
-    @pl.when(step >= q_steps + kv_steps)
-    def _():
-        lin = jnp.dot(h_ref[...], wv_ref[...], preferred_element_type=jnp.float32)
-        v_ref[...] = (lin + bv_ref[...].astype(jnp.float32)).astype(jnp.bfloat16)
-
-
-def project_qkv(tokens, gain, bias, w_query, b_query, w_key, b_key, w_value, b_value, positions):
-    rows, d_model = tokens.shape
-    q_dim, kv_dim = w_query.shape[1], w_key.shape[1]
-    q_steps, kv_steps = q_dim // TILE, kv_dim // TILE
-    half_dim = LANES // 2
-    inv_freq = ROPE_BASE ** (jnp.arange(half_dim, dtype=jnp.float32) * (-2.0 / LANES))
-    angles = positions.astype(jnp.float32)[:, None] * inv_freq[None, :]
-    cos_half, sin_half = jnp.cos(angles), jnp.sin(angles)
-    cos_tab = jnp.concatenate([cos_half, cos_half], axis=-1)
-    sin_tab = jnp.concatenate([-sin_half, sin_half], axis=-1)
-
-    def at_q(i):
-        return 0, jnp.minimum(i, q_steps - 1)
-
-    def at_k(i):
-        return 0, jnp.clip(i - q_steps, 0, kv_steps - 1)
-
-    def at_v(i):
-        return 0, jnp.clip(i - q_steps - kv_steps, 0, kv_steps - 1)
-
-    def whole(shape):
-        return pl.BlockSpec(shape, lambda i: (0, 0))
-
-    return pl.pallas_call(
-        functools.partial(qkv_kernel, q_steps, kv_steps),
-        name='project_qkv',
-        grid=(q_steps + 2 * kv_steps,),
-        out_shape=(jax.ShapeDtypeStruct((rows, q_dim), jnp.bfloat16), jax.ShapeDtypeStruct((rows, kv_dim), jnp.bfloat16), jax.ShapeDtypeStruct((rows, kv_dim), jnp.bfloat16)),
-        in_specs=[whole((rows, d_model)), whole((1, d_model)), whole((1, d_model)),
-                  pl.BlockSpec((d_model, TILE), at_q), pl.BlockSpec((d_model, TILE), at_k), pl.BlockSpec((d_model, TILE), at_v),
-                  pl.BlockSpec((1, TILE), at_q), pl.BlockSpec((1, TILE), at_k), pl.BlockSpec((1, TILE), at_v),
-                  whole((rows, LANES)), whole((rows, LANES))],
-        out_specs=(pl.BlockSpec((rows, TILE), at_q), pl.BlockSpec((rows, TILE), at_k), pl.BlockSpec((rows, TILE), at_v)),
-        scratch_shapes=[pltpu.VMEM((rows, d_model), jnp.bfloat16)],
-    )(tokens, gain[None], bias[None], w_query, w_key, w_value, b_query[None], b_key[None], b_value[None], cos_tab, sin_tab)
-
-
-def attend_kernel(order_ref, pos_ref, span_ref, q_ref, kn_ref, vn_ref, k_hbm, v_hbm, o_ref, k_buf, v_buf, where_ref, sems):
-    groups = order_ref.shape[0] // GROUP
-    heads = q_ref.shape[1]
-    kv_heads = k_hbm.shape[1] // (k_hbm.shape[1] // 4)
+    return centered * lax.rsqrt(var_val + LN_EPS) * gain + bias
+
+
+def attend_kernel(kv_heads, order_ref, pos_ref, span_ref, x_ref, par_ref, rot_ref, meta_ref, wr_ref, wq_hbm, wk_hbm, wv_hbm, wo_hbm, k_hbm, v_hbm,
+                  k_out, v_out, x_out, h_out, gate_out, w_buf, k_buf, v_buf, q_all, kn_all, vn_all, o_all, h_buf, where_ref, w_sem, o_sem, kv_sem):
+    rows, d_model = x_ref.shape
+    heads = q_all.shape[1]
+    share = heads // kv_heads
+    groups = rows // GROUP
     spans = k_hbm.shape[1] // (CHUNK * kv_heads)
+    q_tiles = wq_hbm.shape[1] // TILE
     scale = LANES ** -0.5
-    col = lax.broadcasted_iota(jnp.int32, where_ref.shape, 1)
-    row = lax.broadcasted_iota(jnp.int32, where_ref.shape, 0)
-    where_ref[...] = jnp.where(col % kv_heads == row // (heads // kv_heads), col // kv_heads, 1 << 20)
+
+    def weights(w_hbm, tile, slot):
+        return [pltpu.make_async_copy(w_hbm.at[pl.ds(half * HALF, HALF), pl.ds(tile * TILE, TILE)], w_buf.at[slot + half], w_sem.at[slot + half]) for half in range(2)]
+
+    loads = [weights(wq_hbm, i, 2 * i) for i in range(q_tiles)] + [weights(wk_hbm, 0, 2 * q_tiles), weights(wv_hbm, 0, 2 * q_tiles + 2)]
+    for pair in loads:
+        for copy in pair:
+            copy.start()
 
     def copies(g, n):
         slot = lax.rem(g, DEPTH)
         size = n * CHUNK * kv_heads
         for j in range(GROUP):
             t = order_ref[g * GROUP + j]
-            yield pltpu.make_async_copy(k_hbm.at[t, pl.ds(0, size)], k_buf.at[slot, j, pl.ds(0, size)], sems.at[slot, 0])
-            yield pltpu.make_async_copy(v_hbm.at[t, pl.ds(0, size)], v_buf.at[slot, j, pl.ds(0, size)], sems.at[slot, 1])
+            yield pltpu.make_async_copy(k_hbm.at[t, pl.ds(0, size)], k_buf.at[slot, j, pl.ds(0, size)], kv_sem.at[slot, 0])
+            yield pltpu.make_async_copy(v_hbm.at[t, pl.ds(0, size)], v_buf.at[slot, j, pl.ds(0, size)], kv_sem.at[slot, 1])
 
     def each_span(g, body):
         for n in range(1, spans + 1):
@@ -127,6 +73,46 @@
     for g in range(DEPTH - 1):
         fetch(jnp.int32(g))
 
+    col = lax.broadcasted_iota(jnp.int32, where_ref.shape, 1)
+    row = lax.broadcasted_iota(jnp.int32, where_ref.shape, 0)
+    where_ref[...] = jnp.where(col % kv_heads == (row // share) % kv_heads, col // kv_heads, 1 << 20)
+    h_buf[...] = normed(x_ref[...].astype(jnp.float32), par_ref[0:1, :], par_ref[1:2, :]).astype(jnp.bfloat16)
+
+    def product(index, bias_at):
+        slot = 2 * index
+        for copy in loads[index]:
+            copy.wait()
+        lin = jnp.dot(h_buf[:, :HALF], w_buf[slot], preferred_element_type=jnp.float32) + jnp.dot(h_buf[:, HALF:], w_buf[slot + 1], preferred_element_type=jnp.float32)
+        return lin + par_ref[5:6, bias_at:bias_at + TILE]
+
+    def turned(head):
+        return (head * rot_ref[0] + pltpu.roll(head, LANES // 2, 1) * rot_ref[1]).astype(jnp.bfloat16)
+
+    for i in range(q_tiles):
+        lin = product(i, i * TILE)
+        for n in range(TILE // LANES):
+            q_all[:, i * (TILE // LANES) + n, :] = turned(lin[:, n * LANES:(n + 1) * LANES]).astype(jnp.float32)
+    lin = product(q_tiles, q_tiles * TILE)
+    for n in range(kv_heads):
+        val = turned(lin[:, n * LANES:(n + 1) * LANES])
+        k_out[:, n * LANES:(n + 1) * LANES] = val
+        for m in range(share):
+            kn_all[:, n * share + m, :] = val.astype(jnp.float32)
+    lin = product(q_tiles + 1, (q_tiles + 1) * TILE)
+    for n in range(kv_heads):
+        val = lin[:, n * LANES:(n + 1) * LANES].astype(jnp.bfloat16)
+        v_out[:, n * LANES:(n + 1) * LANES] = val
+        for m in range(share):
+            vn_all[:, n * share + m, :] = val.astype(jnp.float32)
+
+    def out_weights(tile):
+        return pltpu.make_async_copy(wo_hbm.at[:, pl.ds(pl.multiple_of(tile * TILE, TILE), TILE)], w_buf.at[tile], o_sem.at[tile])
+
+    for tile in range(d_model // TILE):
+        out_weights(tile).start()
+
+    block = lax.broadcasted_iota(jnp.int32, (PART * heads, 1), 0) // heads
+
     @pl.loop(0, groups)
     def _(g):
         @pl.when(g + DEPTH - 1 < groups)
@@ -139,26 +125,64 @@
             size = n * CHUNK * kv_heads
             for copy in copies(g, n):
                 copy.wait()
-            for j in range(GROUP):
-                t = order_ref[g * GROUP + j]
-                pos = pos_ref[g * GROUP + j]
-                q_val = q_ref[t]
-                s_val = lax.dot_general(q_val, k_buf[slot, j, :size], (((1,), (1,)), ((), ())), preferred_element_type=jnp.float32) * scale
-                s_new = jnp.sum(q_val.astype(jnp.float32) * kn_ref[t].astype(jnp.float32), axis=1, keepdims=True) * scale
+            for lo in range(0, GROUP, PART):
+                toks = [order_ref[g * GROUP + lo + j] for j in range(PART)]
+                q_rows = [q_all[t] for t in toks]
+                s_val = jnp.concatenate([lax.dot_general(q_rows[j].astype(jnp.bfloat16), k_buf[slot, lo + j, :size], ALONG, preferred_element_type=jnp.float32) for j in range(PART)], axis=0) * scale
+                q_val = jnp.concatenate(q_rows, axis=0)
+                kn_val = jnp.concatenate([kn_all[t] for t in toks], axis=0)
+                vn_val = jnp.concatenate([vn_all[t] for t in toks], axis=0)
+                s_new = jnp.sum(q_val * kn_val, axis=1, keepdims=True) * scale
+                pos = jnp.zeros((PART * heads, 1), jnp.int32)
+                for j in range(PART):
+                    pos = jnp.where(block == j, pos_ref[g * GROUP + lo + j], pos)
                 s_val = jnp.where(where_ref[:, :size] < pos, s_val, -jnp.inf)
                 top = jnp.maximum(jnp.max(s_val, axis=1, keepdims=True), s_new)
                 e_val, e_new = jnp.exp(s_val - top), jnp.exp(s_new - top)
                 inv = 1.0 / (jnp.sum(e_val, axis=1, keepdims=True) + e_new)
                 p_val = (e_val * inv).astype(jnp.bfloat16)
                 p_new = (e_new * inv).astype(jnp.bfloat16).astype(jnp.float32)
-                a_val = jnp.dot(p_val, v_buf[slot, j, :size], preferred_element_type=jnp.float32)
-                o_ref[t] = (a_val + p_new * vn_ref[t].astype(jnp.float32)).astype(jnp.bfloat16)
+                a_val = jnp.concatenate([jnp.dot(p_val[j * heads:(j + 1) * heads], v_buf[slot, lo + j, :size], preferred_element_type=jnp.float32) for j in range(PART)], axis=0)
+                a_val = (a_val + p_new * vn_val).astype(jnp.bfloat16).astype(jnp.float32)
+                for j in range(PART):
+                    o_all[toks[j]] = a_val[j * heads:(j + 1) * heads]
         each_span(g, body)
 
-
-def attend(q_val, k_new, v_new, k_cache, v_cache, positions):
+    for n in range(heads):
+        h_buf[:, n * LANES:(n + 1) * LANES] = o_all[:, n, :].astype(jnp.bfloat16)
+
+    @pl.loop(0, d_model // TILE)
+    def _(tile):
+        out_weights(tile).wait()
+        at = pl.ds(pl.multiple_of(tile * TILE, TILE), TILE)
+        acc = jnp.dot(h_buf[:, :heads * LANES], w_buf[tile], preferred_element_type=jnp.float32)
+        x_out[:, at] = (x_ref[:, at].astype(jnp.float32) + acc + par_ref[4:5, at]).astype(jnp.bfloat16)
+
+    h_two = normed(x_out[...].astype(jnp.float32), par_ref[2:3, :], par_ref[3:4, :]).astype(jnp.bfloat16)
+    h_out[:, :d_model] = h_two
+    logits = lax.dot_general(h_two, wr_ref[...], ALONG, preferred_element_type=jnp.float32)
+    experts = logits.shape[1]
+    expert_ids = lax.broadcasted_iota(jnp.int32, logits.shape, 1)
+    pick_one, pick_two = meta_ref[:, experts:experts + 1], meta_ref[:, experts + 1:experts + 2]
+    hit_one, hit_two = expert_ids == pick_one, expert_ids == pick_two
+    keep_one = meta_ref[:, :experts] == 1
+
+    def gate(keep, hit):
+        val = jnp.where(keep, logits, -jnp.inf)
+        e_val = jnp.exp(val - jnp.max(val, axis=1, keepdims=True))
+        return jnp.sum(jnp.where(hit, e_val, 0.0), axis=1, keepdims=True) / jnp.sum(e_val, axis=1, keepdims=True)
+
+    lane = lax.broadcasted_iota(jnp.int32, gate_out.shape, 1)
+    gate_out[...] = jnp.where(lane == 0, gate(keep_one, hit_one), gate(keep_one & jnp.logical_not(hit_one), hit_two))
+    ids = jnp.where(lane == 0, pick_one, jnp.where(lane == 1, pick_two, 0))
+    h_out[:, d_model:] = ids.astype(jnp.float32).astype(jnp.bfloat16)
+
+
+def attention_layer(tokens, k_cache, v_cache, positions, expert_one, expert_two, eligible, ln1_gain, ln1_bias, w_query, b_query, w_key, b_key, w_value, b_value, w_out, b_out, ln2_gain, ln2_bias, w_router):
     rows, seq_len, kv_heads, head_dim = k_cache.shape
-    heads = q_val.shape[1] // head_dim
+    d_model = tokens.shape[1]
+    heads = w_query.shape[1] // head_dim
+    kv_dim = kv_heads * head_dim
     ids = jnp.arange(rows, dtype=jnp.int32)
     ahead = (positions[None, :] < positions[:, None]) | ((positions[None, :] == positions[:, None]) & (ids[None, :] < ids[:, None]))
     rank = jnp.sum(ahead.astype(jnp.int32), axis=1)
@@ -166,80 +190,38 @@
     order = jnp.sum(jnp.where(hit, ids[None, :], 0), axis=1)
     pos_sorted = jnp.sum(jnp.where(hit, positions[None, :], 0), axis=1)
     span = jnp.clip((pos_sorted[GROUP - 1::GROUP] + CHUNK - 1) // CHUNK, 1, seq_len // CHUNK)
-
-    def spread(val):
-        return jnp.repeat(val.reshape(rows, kv_heads, head_dim), heads // kv_heads, axis=1)
-
+    half_dim = head_dim // 2
+    inv_freq = ROPE_BASE ** (jnp.arange(half_dim, dtype=jnp.float32) * (-2.0 / head_dim))
+    angles = positions.astype(jnp.float32)[:, None] * jnp.concatenate([inv_freq, inv_freq])[None, :]
+    sign = jnp.where(jnp.arange(head_dim) < half_dim, -1.0, 1.0).astype(jnp.float32)
+    rot = jnp.stack([jnp.cos(angles), jnp.sin(angles) * sign[None, :]])
+    biases = jnp.concatenate([b_query, b_key, b_value, jnp.zeros((d_model - heads * head_dim - 2 * kv_dim,), jnp.bfloat16)])
+    par = jnp.stack([ln1_gain, ln1_bias, ln2_gain, ln2_bias, b_out, biases, biases, biases]).astype(jnp.float32)
+    meta = jnp.concatenate([eligible, expert_one[:, None], expert_two[:, None], jnp.zeros((rows, LANES - 2 - eligible.shape[1]), jnp.int32)], axis=1)
     vmem = pl.BlockSpec(memory_space=pltpu.VMEM)
     smem = pl.BlockSpec(memory_space=pltpu.SMEM)
     hbm = pl.BlockSpec(memory_space=pl.ANY)
     flat = (rows, seq_len * kv_heads, head_dim)
+    spread = pltpu.VMEM((rows, heads, head_dim), jnp.float32)
     return pl.pallas_call(
-        attend_kernel,
-        name='attend',
-        out_shape=jax.ShapeDtypeStruct((rows, heads, head_dim), jnp.bfloat16),
-        in_specs=[smem, smem, smem, vmem, vmem, vmem, hbm, hbm],
-        out_specs=vmem,
+        functools.partial(attend_kernel, kv_heads),
+        name='attention_layer',
+        out_shape=(jax.ShapeDtypeStruct((rows, kv_dim), jnp.bfloat16), jax.ShapeDtypeStruct((rows, kv_dim), jnp.bfloat16),
+                   jax.ShapeDtypeStruct((rows, d_model), jnp.bfloat16), jax.ShapeDtypeStruct((rows, d_model + LANES), jnp.bfloat16),
+                   jax.ShapeDtypeStruct((rows, LANES), jnp.float32)),
+        in_specs=[smem, smem, smem, vmem, vmem, vmem, vmem, vmem, hbm, hbm, hbm, hbm, hbm, hbm],
+        out_specs=(vmem,) * 5,
         scratch_shapes=[
+            pltpu.VMEM((2 * (heads * head_dim + 2 * kv_dim) // TILE, HALF, TILE), jnp.bfloat16),
             pltpu.VMEM((DEPTH, GROUP) + flat[1:], jnp.bfloat16), pltpu.VMEM((DEPTH, GROUP) + flat[1:], jnp.bfloat16),
-            pltpu.VMEM((heads, flat[1]), jnp.int32),
+            spread, spread, spread, spread,
+            pltpu.VMEM((rows, d_model), jnp.bfloat16),
+            pltpu.VMEM((PART * heads, flat[1]), jnp.int32),
+            pltpu.SemaphoreType.DMA((2 * (heads * head_dim + 2 * kv_dim) // TILE,)),
+            pltpu.SemaphoreType.DMA((d_model // TILE,)),
             pltpu.SemaphoreType.DMA((DEPTH, 2))],
-        compiler_params=pltpu.CompilerParams(vmem_limit_bytes=48 * 1024 * 1024),
-    )(order, pos_sorted, span, q_val.reshape(rows, heads, head_dim), spread(k_new), spread(v_new), k_cache.reshape(flat), v_cache.reshape(flat))
-
-
-def mix_kernel(a_ref, w_ref, x_ref, b_ref, gain_ref, bias_ref, wr_ref, pick_ref, elig_ref, ids_ref, x_out, h_out, gate_out, x_all):
-    step = pl.program_id(0)
-    width = w_ref.shape[1]
-    d_model = x_all.shape[1]
-    acc = jnp.dot(a_ref[...], w_ref[...], preferred_element_type=jnp.float32)
-    x_mid = (x_ref[...].astype(jnp.float32) + acc + b_ref[...].astype(jnp.float32)).astype(jnp.bfloat16)
-    x_out[...] = x_mid
-    x_all[:, pl.ds(pl.multiple_of(step * width, width), width)] = x_mid
-
-    @pl.when(step == pl.num_programs(0) - 1)
-    def _():
-        h_two = normed(x_all[...].astype(jnp.float32), gain_ref, bias_ref).astype(jnp.bfloat16)
-        h_out[:, :d_model] = h_two
-        h_out[:, d_model:] = ids_ref[...]
-        logits = lax.dot_general(h_two, wr_ref[...], (((1,), (1,)), ((), ())), preferred_element_type=jnp.float32)
-        experts = lax.broadcasted_iota(jnp.int32, logits.shape, 1)
-        hit_one = experts == pick_ref[:, 0:1]
-        hit_two = experts == pick_ref[:, 1:2]
-        keep_one = elig_ref[...] == 1
-
-        def gate(keep, hit):
-            val = jnp.where(keep, logits, -jnp.inf)
-            e_val = jnp.exp(val - jnp.max(val, axis=1, keepdims=True))
-            return jnp.sum(jnp.where(hit, e_val, 0.0), axis=1, keepdims=True) / jnp.sum(e_val, axis=1, keepdims=True)
-
-        lane = lax.broadcasted_iota(jnp.int32, gate_out.shape, 1)
-        gate_out[...] = jnp.where(lane == 0, gate(keep_one, hit_one), gate(keep_one & jnp.logical_not(hit_one), hit_two))
-
-
-def mix(attn, w_out, tokens, b_out, gain, bias, w_router, expert_one, expert_two, eligible):
-    rows, d_model = tokens.shape
-    inner = w_out.shape[0]
-    width = 2 * TILE
-    picks = jnp.stack([expert_one, expert_two], axis=1)
-    ids = jnp.pad(picks.astype(jnp.bfloat16), ((0, 0), (0, LANES - 2)))
-
-    def whole(shape):
-        return pl.BlockSpec(shape, lambda i: (0, 0))
-
-    def tile(height):
-        return pl.BlockSpec((height, width), lambda i: (0, i))
-
-    return pl.pallas_call(
-        mix_kernel,
-        name='mix',
-        grid=(d_model // width,),
-        out_shape=(jax.ShapeDtypeStruct((rows, d_model), jnp.bfloat16), jax.ShapeDtypeStruct((rows, d_model + LANES), jnp.bfloat16), jax.ShapeDtypeStruct((rows, LANES), jnp.float32)),
-        in_specs=[whole((rows, inner)), tile(inner), tile(rows), tile(1), whole((1, d_model)), whole((1, d_model)),
-                  whole((w_router.shape[1], d_model)), whole((rows, 2)), whole(eligible.shape), whole((rows, LANES))],
-        out_specs=(tile(rows), whole((rows, d_model + LANES)), whole((rows, LANES))),
-        scratch_shapes=[pltpu.VMEM((rows, d_model), jnp.bfloat16)],
-    )(attn, w_out, tokens, b_out[None], gain[None], bias[None], w_router.T, picks, eligible, ids)
+        compiler_params=pltpu.CompilerParams(vmem_limit_bytes=62 * 1024 * 1024),
+    )(order, pos_sorted, span, tokens, par, rot, meta, w_router.T, w_query, w_key, w_value, w_out, k_cache.reshape(flat), v_cache.reshape(flat))
 
 
 def flip(me, bit):
@@ -517,9 +499,7 @@
 def solution(mesh):
     def local_step(tokens, k_cache, v_cache, positions, expert_one, expert_two, eligible, ln1_gain, ln1_bias, w_query, b_query, w_key, b_key, w_value, b_value, w_out, b_out, ln2_gain, ln2_bias, w_router, w_gate, w_up, w_down):
         rows, seq_len, kv_heads, head_dim = k_cache.shape
-        q_val, k_val, v_val = project_qkv(tokens, ln1_gain, ln1_bias, w_query, b_query, w_key, b_key, w_value, b_value, positions)
-        attn = attend(q_val, k_val, v_val, k_cache, v_cache, positions).reshape(rows, -1)
-        x_mid, h_ext, gates = mix(attn, w_out, tokens, b_out, ln2_gain, ln2_bias, w_router, expert_one, expert_two, eligible)
+        k_val, v_val, x_mid, h_ext, gates = attention_layer(tokens, k_cache, v_cache, positions, expert_one, expert_two, eligible, ln1_gain, ln1_bias, w_query, b_query, w_key, b_key, w_value, b_value, w_out, b_out, ln2_gain, ln2_bias, w_router)
         z_val, ids = gather_and_activate(h_ext, w_gate[0].T, w_up[0].T)
         rel = ids[:, :rows].astype(jnp.int32) ^ lax.axis_index('ep')
         tokens_out = project_and_return(z_val, w_down[0], rel, gates, x_mid)

time: 303 us -> 262 us (0.86)
  Pallas kernels: 280 us -> 243 us
  local copies, waits for them, and re-layouts: 17.2 us -> 9.94 us
  other arithmetic: 3.86 us -> 8.4 us
    pallas_call x3 -> x1, Pallas kernels: 80 us -> 42.2 us  [attention_layer(): pl.pallas_call(functools.partial(attend_kernel, kv_heads), name='attentio...]
    broadcast_in_dim x10 -> x4, local copies, waits for them, and re-layouts: 8.59 us -> 1.53 us  [the longest x1 0.76 us: attention_layer(): expert_one[:, None]]
    another operation x1 -> x7, local copies, waits for them, and re-layouts: 0.73 us -> 3.76 us  [attention_layer(): jnp.stack([ln1_gain, ln1_bias, ln2_gain, ln2_bias, b_out, biases, biases,...]
where the time goes in v4:
time: 262 us
  Pallas kernels  243 us (93%)
  local copies, waits for them, and re-layouts  9.94 us (4%)
  other arithmetic  8.4 us (3%)
    pallas_call x1, Pallas kernels, project_and_return(): pl.pallas_call(return_kernel, name='return_rows', out_shape=jax.ShapeDtyp...  124 us
    pallas_call x1, Pallas kernels, gather_and_activate(): pl.pallas_call(functools.partial(gather_kernel, bounds), name='gather_row...  76.2 us
    pallas_call x1, Pallas kernels, attention_layer(): pl.pallas_call(functools.partial(attend_kernel, kv_heads), name='attentio...  42.2 us

profile of v4, /device:TPU:0, one launch (start us, length us, event | category | flops | bytes accessed | tf_op | source)
XLA Modules:
  0.0 261.6 jit_solution(6639768881173228240)
XLA Ops:
  0.7 0.7 convert_element_type.14
  1.4 0.3 multiply_cosine_fusion
  1.7 0.7 pad_maximum_fusion.rot_ref
  2.4 0.8 copy.29
  3.2 0.8 copy.30
  3.9 0.8 copy.31
  4.8 0.9 convert_reduce_fusion
  5.7 2.0 select_reduce_fusion
  7.8 0.5 fusion.3.span_ref
  8.3 0.7 pad_maximum_fusion.1
  9.1 0.7 stack.28
  9.8 0.7 stack.29
  10.5 0.7 stack.30
  11.2 0.7 stack.31
  11.9 0.7 stack.32
  12.6 0.2 stack.34
  12.8 0.7 convert_element_type.13.par_ref
  13.5 42.2 %attention_layer.1 = (bf16[128,512]{1,0:T(8,128)(2,1)}, bf16[128,512]{1,0:T(8,128)(2,1)}, bf16[128,4096]{1,0:T(8,128)(2,1)}, bf16[128,4224]{1,0:T(8,128)(2,1)}, f32[128,128]{1,0:T(8,128)}) custom-call(s32[128]{0:T(128)} %get-tuple-element.18.order_ref, s32[128]{0:T(128)} %copy-done.2, s32[16]{0:T(128)} %fusion.3.span_ref, bf16[128,4096]{1,0:T(8,128)(2,1)} %x_ref.1, ...), custom_call_target="tpu_custom_call" | custom-call | tf_op jit(solution)/shard_map/attention_layer/pallas_call | solution.py:206
  55.8 76.2 %gather_rows.1 = (bf16[8,256,448]{2,1,0:T(8,128)(2,1)}, bf16[8,256,128]{2,1,0:T(8,128)(2,1)}) custom-call(bf16[128,4224]{1,0:T(8,128)(2,1)} %get-tuple-element.10.h_ref, bf16[448,4096]{1,0:T(8,128)(2,1)} %bitcast.14, bf16[448,4096]{1,0:T(8,128)(2,1)} %bitcast.15), custom_call_target="tpu_custom_call" | custom-call | tf_op jit(solution)/shard_map/gather_rows/pallas_call | solution.py:461
  131.9 1.8 convert_xor_fusion.rel_ref
  133.8 124.2 %return_rows.1 = bf16[128,4096]{1,0:T(8,128)(2,1)} custom-call(bf16[8,256,448]{2,1,0:T(8,128)(2,1)} %get-tuple-element.11.z_ref, bf16[448,4096]{1,0:T(8,128)(2,1)} %bitcast.16, s32[8,128,128]{2,1,0:T(8,128)} %convert_xor_fusion.rel_ref, f32[128,128]{1,0:T(8,128)} %get-tuple-element.13.gate_ref, bf16[128,4096]{1,0:T(8,128)(2,1)} %get-tuple-element.14.x_ref), custom_call_target="tpu_custom_call" | custom-call | tf_op jit(solution)/shard_map/return_rows/pallas_call | solution.py:479
  258.0 0.7 reshape.137
  258.6 0.7 reshape.138
  259.3 2.3 copy.33
  (13 shorter events, 0.3 us)
Async XLA Ops:
  7.7 5.8 %copy-start.2 = (s32[128]{0:T(128)}, s32[128]{0:T(128)S(1)}, u32[]{:S(2)}) copy-start(s32[128]{0:T(128)S(1)} %get-tuple-element.17.pos_ref) | copy-start | bytes 1540
  133.8 124.2 %copy-start.1 = (bf16[128,512]{1,0:T(8,128)(2,1)S(1)}, bf16[128,512]{1,0:T(8,128)(2,1)}, u32[]{:S(2)}) copy-start(bf16[128,512]{1,0:T(8,128)(2,1)} %get-tuple-element.15) | copy-start | bytes 393220
  133.8 124.9 %copy-start = (bf16[128,512]{1,0:T(8,128)(2,1)S(1)}, bf16[128,512]{1,0:T(8,128)(2,1)}, u32[]{:S(2)}) copy-start(bf16[128,512]{1,0:T(8,128)(2,1)} %get-tuple-element.16) | copy-start | bytes 393220

commit v5 on v4

--- a/solution.py
+++ b/solution.py
@@ -25,6 +25,10 @@
 CHUNK = 64
 
 
+def row_of(ref):
+    return jnp.concatenate([ref[i:i + 1, :] for i in range(ref.shape[0])], axis=1).astype(jnp.float32)
+
+
 def normed(x_f, gain, bias):
     mean_val = jnp.mean(x_f, axis=-1, keepdims=True)
     centered = x_f - mean_val
@@ -32,7 +36,7 @@
     return centered * lax.rsqrt(var_val + LN_EPS) * gain + bias
 
 
-def attend_kernel(kv_heads, order_ref, pos_ref, span_ref, x_ref, par_ref, rot_ref, meta_ref, wr_ref, wq_hbm, wk_hbm, wv_hbm, wo_hbm, k_hbm, v_hbm,
+def attend_kernel(kv_heads, order_ref, pos_ref, span_ref, x_ref, g1_ref, c1_ref, g2_ref, c2_ref, bo_ref, bq_ref, bk_ref, bv_ref, rot_ref, elig_ref, one_ref, two_ref, wr_ref, wq_hbm, wk_hbm, wv_hbm, wo_hbm, k_hbm, v_hbm,
                   k_out, v_out, x_out, h_out, gate_out, w_buf, k_buf, v_buf, q_all, kn_all, vn_all, o_all, h_buf, where_ref, w_sem, o_sem, kv_sem):
     rows, d_model = x_ref.shape
     heads = q_all.shape[1]
@@ -76,29 +80,30 @@
     col = lax.broadcasted_iota(jnp.int32, where_ref.shape, 1)
     row = lax.broadcasted_iota(jnp.int32, where_ref.shape, 0)
     where_ref[...] = jnp.where(col % kv_heads == (row // share) % kv_heads, col // kv_heads, 1 << 20)
-    h_buf[...] = normed(x_ref[...].astype(jnp.float32), par_ref[0:1, :], par_ref[1:2, :]).astype(jnp.bfloat16)
-
-    def product(index, bias_at):
+    h_buf[...] = normed(x_ref[...].astype(jnp.float32), row_of(g1_ref), row_of(c1_ref)).astype(jnp.bfloat16)
+
+    def product(index, bias):
         slot = 2 * index
         for copy in loads[index]:
             copy.wait()
         lin = jnp.dot(h_buf[:, :HALF], w_buf[slot], preferred_element_type=jnp.float32) + jnp.dot(h_buf[:, HALF:], w_buf[slot + 1], preferred_element_type=jnp.float32)
-        return lin + par_ref[5:6, bias_at:bias_at + TILE]
+        return lin + bias
 
     def turned(head):
         return (head * rot_ref[0] + pltpu.roll(head, LANES // 2, 1) * rot_ref[1]).astype(jnp.bfloat16)
 
+    bq_row = row_of(bq_ref)
     for i in range(q_tiles):
-        lin = product(i, i * TILE)
+        lin = product(i, bq_row[:, i * TILE:(i + 1) * TILE])
         for n in range(TILE // LANES):
             q_all[:, i * (TILE // LANES) + n, :] = turned(lin[:, n * LANES:(n + 1) * LANES]).astype(jnp.float32)
-    lin = product(q_tiles, q_tiles * TILE)
+    lin = product(q_tiles, row_of(bk_ref))
     for n in range(kv_heads):
         val = turned(lin[:, n * LANES:(n + 1) * LANES])
         k_out[:, n * LANES:(n + 1) * LANES] = val
         for m in range(share):
             kn_all[:, n * share + m, :] = val.astype(jnp.float32)
-    lin = product(q_tiles + 1, (q_tiles + 1) * TILE)
+    lin = product(q_tiles + 1, row_of(bv_ref))
     for n in range(kv_heads):
         val = lin[:, n * LANES:(n + 1) * LANES].astype(jnp.bfloat16)
         v_out[:, n * LANES:(n + 1) * LANES] = val
@@ -106,7 +111,7 @@
             vn_all[:, n * share + m, :] = val.astype(jnp.float32)
 
     def out_weights(tile):
-        return pltpu.make_async_copy(wo_hbm.at[:, pl.ds(pl.multiple_of(tile * TILE, TILE), TILE)], w_buf.at[tile], o_sem.at[tile])
+        return pltpu.make_async_copy(wo_hbm.at[:, pl.ds(tile * TILE, TILE)], w_buf.at[tile], o_sem.at[tile])
 
     for tile in range(d_model // TILE):
         out_weights(tile).start()
@@ -151,21 +156,23 @@
     for n in range(heads):
         h_buf[:, n * LANES:(n + 1) * LANES] = o_all[:, n, :].astype(jnp.bfloat16)
 
-    @pl.loop(0, d_model // TILE)
-    def _(tile):
+    bo_row = row_of(bo_ref)
+    for tile in range(d_model // TILE):
         out_weights(tile).wait()
-        at = pl.ds(pl.multiple_of(tile * TILE, TILE), TILE)
+        at = slice(tile * TILE, (tile + 1) * TILE)
         acc = jnp.dot(h_buf[:, :heads * LANES], w_buf[tile], preferred_element_type=jnp.float32)
-        x_out[:, at] = (x_ref[:, at].astype(jnp.float32) + acc + par_ref[4:5, at]).astype(jnp.bfloat16)
-
-    h_two = normed(x_out[...].astype(jnp.float32), par_ref[2:3, :], par_ref[3:4, :]).astype(jnp.bfloat16)
+        x_out[:, at] = (x_ref[:, at].astype(jnp.float32) + acc + bo_row[:, at]).astype(jnp.bfloat16)
+
+    h_two = normed(x_out[...].astype(jnp.float32), row_of(g2_ref), row_of(c2_ref)).astype(jnp.bfloat16)
     h_out[:, :d_model] = h_two
     logits = lax.dot_general(h_two, wr_ref[...], ALONG, preferred_element_type=jnp.float32)
     experts = logits.shape[1]
     expert_ids = lax.broadcasted_iota(jnp.int32, logits.shape, 1)
-    pick_one, pick_two = meta_ref[:, experts:experts + 1], meta_ref[:, experts + 1:experts + 2]
+    stacked = jnp.concatenate([elig_ref[...], one_ref[...], two_ref[...], jnp.zeros((rows - experts - 2, rows), jnp.int32)], axis=0)
+    meta = stacked.astype(jnp.float32).T.astype(jnp.int32)
+    pick_one, pick_two = meta[:, experts:experts + 1], meta[:, experts + 1:experts + 2]
     hit_one, hit_two = expert_ids == pick_one, expert_ids == pick_two
-    keep_one = meta_ref[:, :experts] == 1
+    keep_one = meta[:, :experts] == 1
 
     def gate(keep, hit):
         val = jnp.where(keep, logits, -jnp.inf)
@@ -195,9 +202,7 @@
     angles = positions.astype(jnp.float32)[:, None] * jnp.concatenate([inv_freq, inv_freq])[None, :]
     sign = jnp.where(jnp.arange(head_dim) < half_dim, -1.0, 1.0).astype(jnp.float32)
     rot = jnp.stack([jnp.cos(angles), jnp.sin(angles) * sign[None, :]])
-    biases = jnp.concatenate([b_query, b_key, b_value, jnp.zeros((d_model - heads * head_dim - 2 * kv_dim,), jnp.bfloat16)])
-    par = jnp.stack([ln1_gain, ln1_bias, ln2_gain, ln2_bias, b_out, biases, biases, biases]).astype(jnp.float32)
-    meta = jnp.concatenate([eligible, expert_one[:, None], expert_two[:, None], jnp.zeros((rows, LANES - 2 - eligible.shape[1]), jnp.int32)], axis=1)
+    small = [p.reshape(-1, LANES) for p in (ln1_gain, ln1_bias, ln2_gain, ln2_bias, b_out, b_query, b_key, b_value)]
     vmem = pl.BlockSpec(memory_space=pltpu.VMEM)
     smem = pl.BlockSpec(memory_space=pltpu.SMEM)
     hbm = pl.BlockSpec(memory_space=pl.ANY)
@@ -209,7 +214,7 @@
         out_shape=(jax.ShapeDtypeStruct((rows, kv_dim), jnp.bfloat16), jax.ShapeDtypeStruct((rows, kv_dim), jnp.bfloat16),
                    jax.ShapeDtypeStruct((rows, d_model), jnp.bfloat16), jax.ShapeDtypeStruct((rows, d_model + LANES), jnp.bfloat16),
                    jax.ShapeDtypeStruct((rows, LANES), jnp.float32)),
-        in_specs=[smem, smem, smem, vmem, vmem, vmem, vmem, vmem, hbm, hbm, hbm, hbm, hbm, hbm],
+        in_specs=[smem, smem, smem] + [vmem] * 14 + [hbm, hbm, hbm, hbm, hbm, hbm],
         out_specs=(vmem,) * 5,
         scratch_shapes=[
             pltpu.VMEM((2 * (heads * head_dim + 2 * kv_dim) // TILE, HALF, TILE), jnp.bfloat16),
@@ -221,7 +226,11 @@
             pltpu.SemaphoreType.DMA((d_model // TILE,)),
             pltpu.SemaphoreType.DMA((DEPTH, 2))],
         compiler_params=pltpu.CompilerParams(vmem_limit_bytes=62 * 1024 * 1024),
-    )(order, pos_sorted, span, tokens, par, rot, meta, w_router.T, w_query, w_key, w_value, w_out, k_cache.reshape(flat), v_cache.reshape(flat))
+    )(order, pos_sorted, span, tokens, *small, rot, eligible.T, expert_one[None], expert_two[None], w_router.T, w_query, w_key, w_value, w_out, k_cache.reshape(flat), v_cache.reshape(flat))
+
+
+def seat(slot):
+    return {3: 4, 4: 3}.get(slot, slot)
 
 
 def flip(me, bit):
@@ -237,7 +246,7 @@
     return me
 
 
-def gather_kernel(bounds, h_ref, wg_ref, wu_ref, z_ref, id_ref, x_a, x_b, x_c, own_sem, send_sem, recv_sem, side_send, side_recv):
+def gather_kernel(bounds, h_ref, wg_hbm, wu_hbm, z_ref, rel_ref, x_a, x_b, x_c, wg_ref, wu_ref, own_sem, send_sem, recv_sem, side_send, side_recv):
     rows = x_a.shape[1] // 2
     bufs = (x_a, x_b, x_c)
     copies = []
@@ -249,43 +258,50 @@
 
     def hop(f, src, bit):
         return pltpu.make_async_remote_copy(
-            src_ref=bufs[f].at[src, pl.ds(0, rows)], dst_ref=bufs[f].at[src ^ bit, pl.ds(0, rows)],
+            src_ref=bufs[f].at[seat(src), pl.ds(0, rows)], dst_ref=bufs[f].at[seat(src ^ bit), pl.ds(0, rows)],
             send_sem=send_sem.at[f, src ^ bit], recv_sem=recv_sem.at[f, src ^ bit],
             device_id=(flip(me, 2 * bit),), device_id_type=MESH)
 
     def side(f, src):
         return pltpu.make_async_remote_copy(
-            src_ref=bufs[f].at[src, pl.ds(0, rows)], dst_ref=bufs[f].at[src, pl.ds(rows, rows)],
+            src_ref=bufs[f].at[seat(src), pl.ds(0, rows)], dst_ref=bufs[f].at[seat(src), pl.ds(rows, rows)],
             send_sem=side_send.at[f, src], recv_sem=side_recv.at[f, src],
             device_id=(flip(me, 1),), device_id_type=MESH)
 
     def landed(f, slot):
         hop(f, 0, slot).wait_recv()
 
-    def activate(pair):
+    def activate(first, count):
         u_val = v_val = None
         for f in range(3):
             lo, hi = bounds[f]
             hi = min(hi, wg_ref.shape[1])
-            x_val = bufs[f][pair, :, : hi - lo]
+            x_val = bufs[f][first:first + count, :, : hi - lo].reshape(2 * rows * count, hi - lo)
             u_part = lax.dot_general(x_val, wg_ref[:, lo:hi], ALONG, preferred_element_type=jnp.float32)
             v_part = lax.dot_general(x_val, wu_ref[:, lo:hi], ALONG, preferred_element_type=jnp.float32)
             u_val = u_part if u_val is None else u_val + u_part
             v_val = v_part if v_val is None else v_val + v_part
-        z_ref[pair] = (jax.nn.silu(u_val) * v_val).astype(jnp.bfloat16)
-        id_ref[pair] = bufs[2][pair, :, pl.ds(bounds[2][1] - bounds[2][0] - LANES, LANES)]
+        z_ref[first:first + count] = (jax.nn.silu(u_val) * v_val).astype(jnp.bfloat16).reshape(count, 2 * rows, -1)
+        for i in range(first, first + count):
+            ids = bufs[2][i, :rows, bounds[2][1] - bounds[2][0] - LANES:]
+            rel_ref[i] = ids.astype(jnp.float32).astype(jnp.int32) ^ me
 
     for f in range(3):
         copies[f].wait()
         hop(f, 0, ORDERS[f][0]).start()
+    weights = [pltpu.make_async_copy(src, dst, own_sem.at[3 + i]) for i, (src, dst) in enumerate(((wg_hbm, wg_ref), (wu_hbm, wu_ref)))]
     for f in range(3):
         side(f, 0).start()
+    for copy in weights:
+        copy.start()
     for stage in (1, 2):
         for f in range(3):
             hop(f, 0, ORDERS[f][stage]).start()
     for f in range(3):
         side(f, 0).wait_recv()
-    activate(0)
+    for copy in weights:
+        copy.wait()
+    activate(0, 1)
     for f in range(3):
         a, b, g = ORDERS[f]
         landed(f, a)
@@ -310,10 +326,7 @@
         for slot in (1, 2, 4):
             side(f, slot).wait_recv()
 
-    @pl.loop(0, 3)
-    def _(i):
-        activate(i * (i + 1) // 2 + 1)
-
+    activate(1, 3)
     for f in range(3):
         a, b, g = ORDERS[f]
         landed(f, a ^ g)
@@ -324,16 +337,13 @@
         for slot in (3, 5, 6):
             side(f, slot).wait_recv()
 
-    @pl.loop(0, 3)
-    def _(i):
-        activate(6 - i * (i + 1) // 2)
-
+    activate(4, 3)
     for f in range(3):
         landed(f, 7)
         side(f, 7).start()
     for f in range(3):
         side(f, 7).wait_recv()
-    activate(7)
+    activate(7, 1)
     for f in range(3):
         for slot in range(8):
             side(f, slot).wait_send()
@@ -353,101 +363,116 @@
     def remote(src, dst, send, recv, bit):
         return pltpu.make_async_remote_copy(src_ref=src, dst_ref=dst, send_sem=send, recv_sem=recv, device_id=(flip(me, bit),), device_id_type=MESH)
 
-    def side(q):
-        return remote(side_buf.at[q], pair_buf.at[q, 1], side_send.at[q], side_recv.at[q], 1)
-
-    def hop_one(f, q):
-        return remote(pair_buf.at[q, :, pl.ds(4 * rows, 4 * rows)], near_buf.at[q], hop_send.at[0, q], hop_recv.at[0, q], 2 * ORDERS[f][0])
-
-    def hop_two(f, q):
-        return remote(turn_buf.at[q], turn_in.at[q], hop_send.at[1, q], hop_recv.at[1, q], 2 * ORDERS[f][1])
-
-    def hop_three(f, q):
-        return remote(last_buf.at[q], last_in.at[q], hop_send.at[2, q], hop_recv.at[2, q], 2 * ORDERS[f][2])
-
-    def project(f, q):
-        w_val = wd_ref[:, pl.ds(pl.multiple_of(q * WIDTH, WIDTH), WIDTH)]
+    def side(part):
+        f, q, s, lo, width = part
+        cols = pl.ds(lo, width)
+        return remote(side_buf.at[q, :, cols], pair_buf.at[q, 1, :, cols], side_send.at[s], side_recv.at[s], 1)
+
+    def hop_one(part):
+        f, q, s, lo, width = part
+        cols = pl.ds(lo, width)
+        return remote(pair_buf.at[q, :, pl.ds(4 * rows, 4 * rows), cols], near_buf.at[q, :, :, cols], hop_send.at[0, s], hop_recv.at[0, s], 2 * ORDERS[f][0])
+
+    def hop_two(part):
+        f, q, s, lo, width = part
+        cols = pl.ds(lo, width)
+        return remote(turn_buf.at[q, :, :, cols], turn_in.at[q, :, :, cols], hop_send.at[1, s], hop_recv.at[1, s], 2 * ORDERS[f][1])
+
+    def hop_three(part):
+        f, q, s, lo, width = part
+        cols = pl.ds(lo, width)
+        return remote(last_buf.at[q, :, :, cols], last_in.at[q, :, :, cols], hop_send.at[2, s], hop_recv.at[2, s], 2 * ORDERS[f][2])
+
+    def project(part):
+        f, q, s, lo, width = part
+        w_val = wd_ref[:, pl.ds(pl.multiple_of(q * WIDTH + lo, LANES), width)]
         for place in range(8):
-            e_val = jnp.dot(z_ref[slot_of(f, place)], w_val, preferred_element_type=jnp.float32).astype(jnp.bfloat16)
-            pair_buf[q, 0, place * rows:(place + 1) * rows, :] = e_val[:rows]
-            side_buf[q, place * rows:(place + 1) * rows, :] = e_val[rows:]
-        side(q).start()
-
-    def send_far(f, q):
-        side(q).wait_recv()
-        hop_one(f, q).start()
-
-    def choose(f, q, place, k, other):
-        rel = rel_ref[slot_of(f, place)][:, k:k + 1]
-        at = pl.ds(place * rows, rows)
+            e_val = jnp.dot(z_ref[seat(slot_of(f, place))], w_val, preferred_element_type=jnp.float32).astype(jnp.bfloat16)
+            pair_buf[q, 0, place * rows:(place + 1) * rows, lo:lo + width] = e_val[:rows]
+            side_buf[q, place * rows:(place + 1) * rows, lo:lo + width] = e_val[rows:]
+        side(part).start()
+
+    def send_far(part):
+        side(part).wait_recv()
+        hop_one(part).start()
+
+    def choose(part, place, k, other):
+        f, q, s, lo, width = part
+        rel = rel_ref[seat(slot_of(f, place))][:, k:k + 1]
+        at, cols = pl.ds(place * rows, rows), pl.ds(lo, width)
         far = 2 * ORDERS[f][0]
-        val = other
-        if val is None:
-            val = near_buf[q, 1, at, :].astype(jnp.float32)
-        else:
-            val = jnp.where(rel == far + 1, near_buf[q, 1, at, :].astype(jnp.float32), val)
-        val = jnp.where(rel == far, near_buf[q, 0, at, :].astype(jnp.float32), val)
-        val = jnp.where(rel == 1, pair_buf[q, 1, at, :].astype(jnp.float32), val)
-        return jnp.where(rel == 0, pair_buf[q, 0, at, :].astype(jnp.float32), val)
-
-    def turn(f, q):
-        hop_one(f, q).wait_recv()
+        val = near_buf[q, 1, at, cols].astype(jnp.float32)
+        if other is not None:
+            val = jnp.where(rel == far + 1, val, other)
+        val = jnp.where(rel == far, near_buf[q, 0, at, cols].astype(jnp.float32), val)
+        val = jnp.where(rel == 1, pair_buf[q, 1, at, cols].astype(jnp.float32), val)
+        return jnp.where(rel == 0, pair_buf[q, 0, at, cols].astype(jnp.float32), val)
+
+    def turn(part):
+        f, q, s, lo, width = part
+        hop_one(part).wait_recv()
         for k in range(2):
             for half in range(2):
-                turn_buf[q, k, half * rows:(half + 1) * rows, :] = choose(f, q, 2 + half, k, None).astype(jnp.bfloat16)
-        hop_two(f, q).start()
-
-    def last(f, q):
-        hop_two(f, q).wait_recv()
+                turn_buf[q, k, half * rows:(half + 1) * rows, lo:lo + width] = choose(part, 2 + half, k, None).astype(jnp.bfloat16)
+        hop_two(part).start()
+
+    def last(part):
+        f, q, s, lo, width = part
+        hop_two(part).wait_recv()
         for k in range(2):
-            other = turn_in[q, k, rows:2 * rows, :].astype(jnp.float32)
-            last_buf[q, k] = choose(f, q, 1, k, other).astype(jnp.bfloat16)
-        hop_three(f, q).start()
-
-    def finish(f, q):
-        hop_three(f, q).wait_recv()
+            other = turn_in[q, k, rows:2 * rows, lo:lo + width].astype(jnp.float32)
+            last_buf[q, k, :, lo:lo + width] = choose(part, 1, k, other).astype(jnp.bfloat16)
+        hop_three(part).start()
+
+    def finish(part):
+        f, q, s, lo, width = part
+        hop_three(part).wait_recv()
         g_bit = 2 * ORDERS[f][2]
         y_val = None
         for k in range(2):
             rel = rel_ref[0][:, k:k + 1]
-            other = jnp.where((rel // g_bit) % 2 == 1, last_in[q, k].astype(jnp.float32), turn_in[q, k, :rows, :].astype(jnp.float32))
-            part = gate_ref[:, k:k + 1] * choose(f, q, 0, k, other)
-            y_val = part if y_val is None else y_val + part
-        at = pl.ds(pl.multiple_of(q * WIDTH, WIDTH), WIDTH)
+            other = jnp.where((rel // g_bit) % 2 == 1, last_in[q, k, :, lo:lo + width].astype(jnp.float32), turn_in[q, k, :rows, lo:lo + width].astype(jnp.float32))
+            add = gate_ref[:, k:k + 1] * choose(part, 0, k, other)
+            y_val = add if y_val is None else y_val + add
+        at = pl.ds(pl.multiple_of(q * WIDTH + lo, LANES), width)
         out_ref[:, at] = (x_ref[:, at].astype(jnp.float32) + y_val).astype(jnp.bfloat16)
 
+    full = chunks // 3
+    tail = [(f, chunks - 1, chunks - 1 + f, f * LANES, LANES) for f in range(2)]
+
+    def body(f, j):
+        return f, 3 * j + f, 3 * j + f, 0, WIDTH
+
     def sweep(step):
-        @pl.loop(0, chunks // 3)
+        @pl.loop(0, full)
         def _(j):
             for f in range(3):
-                step(f, 3 * j + f)
-        for q in range(chunks // 3 * 3, chunks):
-            step(q % 3, q)
-
-    for f in range(3):
-        project(f, f)
-
-    @pl.loop(1, chunks // 3)
+                step(body(f, j))
+        for part in tail:
+            step(part)
+
+    for f in range(3):
+        project(body(f, 0))
+
+    @pl.loop(1, full)
     def _(j):
         for f in range(3):
-            project(f, 3 * j + f)
-            send_far(f, 3 * j + f - 3)
-
-    for q in range(chunks // 3 * 3, chunks):
-        project(q % 3, q)
-    for f in range(3):
-        send_far(f, chunks // 3 * 3 - 3 + f)
-    for q in range(chunks // 3 * 3, chunks):
-        send_far(q % 3, q)
+            project(body(f, j))
+            send_far(body(f, j - 1))
+
+    for part in tail:
+        project(part)
+    for part in [body(f, full - 1) for f in range(3)] + tail:
+        send_far(part)
     sweep(turn)
     sweep(last)
     sweep(finish)
 
-    def drain(f, q):
-        side(q).wait_send()
-        hop_one(f, q).wait_send()
-        hop_two(f, q).wait_send()
-        hop_three(f, q).wait_send()
+    def drain(part):
+        side(part).wait_send()
+        hop_one(part).wait_send()
+        hop_two(part).wait_send()
+        hop_three(part).wait_send()
     sweep(drain)
 
 
@@ -461,11 +486,12 @@
     return pl.pallas_call(
         functools.partial(gather_kernel, bounds),
         name='gather_rows',
-        out_shape=(jax.ShapeDtypeStruct((8, 2 * rows, d_ff), jnp.bfloat16), jax.ShapeDtypeStruct((8, 2 * rows, LANES), jnp.bfloat16)),
-        in_specs=[pl.BlockSpec(memory_space=pl.ANY), vmem, vmem],
+        out_shape=(jax.ShapeDtypeStruct((8, 2 * rows, d_ff), jnp.bfloat16), jax.ShapeDtypeStruct((8, rows, LANES), jnp.int32)),
+        in_specs=[pl.BlockSpec(memory_space=pl.ANY)] * 3,
         out_specs=(vmem, vmem),
         scratch_shapes=[pltpu.VMEM((8, 2 * rows, hi - lo), jnp.bfloat16) for lo, hi in bounds] + [
-            pltpu.SemaphoreType.DMA((3,)),
+            pltpu.VMEM(w_gate.shape, jnp.bfloat16), pltpu.VMEM(w_gate.shape, jnp.bfloat16),
+            pltpu.SemaphoreType.DMA((5,)),
             pltpu.SemaphoreType.DMA((3, 8)), pltpu.SemaphoreType.DMA((3, 8)),
             pltpu.SemaphoreType.DMA((3, 8)), pltpu.SemaphoreType.DMA((3, 8))],
         compiler_params=pltpu.CompilerParams(collective_id=0, has_side_effects=True, vmem_limit_bytes=60 * 1024 * 1024),
@@ -490,8 +516,8 @@
             pltpu.VMEM((chunks, 2, 2 * rows, WIDTH), jnp.bfloat16),
             pltpu.VMEM((chunks, 2, rows, WIDTH), jnp.bfloat16),
             pltpu.VMEM((chunks, 2, rows, WIDTH), jnp.bfloat16),
-            pltpu.SemaphoreType.DMA((chunks,)), pltpu.SemaphoreType.DMA((chunks,)),
-            pltpu.SemaphoreType.DMA((3, chunks)), pltpu.SemaphoreType.DMA((3, chunks))],
+            pltpu.SemaphoreType.DMA((chunks + 1,)), pltpu.SemaphoreType.DMA((chunks + 1,)),
+            pltpu.SemaphoreType.DMA((3, chunks + 1)), pltpu.SemaphoreType.DMA((3, chunks + 1))],
         compiler_params=pltpu.CompilerParams(collective_id=1, has_side_effects=True, vmem_limit_bytes=63 * 1024 * 1024),
     )(z_val, w_down, rel, gates, x_mid)
 
@@ -500,8 +526,7 @@
     def local_step(tokens, k_cache, v_cache, positions, expert_one, expert_two, eligible, ln1_gain, ln1_bias, w_query, b_query, w_key, b_key, w_value, b_value, w_out, b_out, ln2_gain, ln2_bias, w_router, w_gate, w_up, w_down):
         rows, seq_len, kv_heads, head_dim = k_cache.shape
         k_val, v_val, x_mid, h_ext, gates = attention_layer(tokens, k_cache, v_cache, positions, expert_one, expert_two, eligible, ln1_gain, ln1_bias, w_query, b_query, w_key, b_key, w_value, b_value, w_out, b_out, ln2_gain, ln2_bias, w_router)
-        z_val, ids = gather_and_activate(h_ext, w_gate[0].T, w_up[0].T)
-        rel = ids[:, :rows].astype(jnp.int32) ^ lax.axis_index('ep')
+        z_val, rel = gather_and_activate(h_ext, w_gate[0].T, w_up[0].T)
         tokens_out = project_and_return(z_val, w_down[0], rel, gates, x_mid)
         key_new, value_new = k_val.reshape(rows, kv_heads, head_dim), v_val.reshape(rows, kv_heads, head_dim)
         return tokens_out, key_new, value_new

time: 262 us -> 248 us (0.947)
  Pallas kernels: 243 us -> 237 us
  local copies, waits for them, and re-layouts: 9.94 us -> 5.58 us
  other arithmetic: 8.4 us -> 4.44 us
    another operation x7 -> x0, local copies, waits for them, and re-layouts: 3.76 us -> none  [attention_layer(): jnp.stack([ln1_gain, ln1_bias, ln2_gain, ln2_bias, b_out, biases, biases,...]
    pallas_call x1, Pallas kernels: 76.2 us -> 72.6 us  [gather_and_activate(): pl.pallas_call(functools.partial(gather_kernel, bounds), name='gather_row...]
where the time goes in v5:
time: 248 us
  Pallas kernels  237 us (96%)
  local copies, waits for them, and re-layouts  5.58 us (2%)
  other arithmetic  4.44 us (2%)
    pallas_call x1, Pallas kernels, project_and_return(): pl.pallas_call(return_kernel, name='return_rows', out_shape=jax.ShapeDtyp...  122 us
    pallas_call x1, Pallas kernels, gather_and_activate(): pl.pallas_call(functools.partial(gather_kernel, bounds), name='gather_row...  72.6 us
    pallas_call x1, Pallas kernels, attention_layer(): pl.pallas_call(functools.partial(attend_kernel, kv_heads), name='attentio...  42.7 us

profile of v5, /device:TPU:0, one launch (start us, length us, event | category | flops | bytes accessed | tf_op | source)
XLA Modules:
  0.0 248.0 jit_solution(17509784679533062764)
XLA Ops:
  0.6 0.7 convert_element_type.7
  1.3 0.9 convert_reduce_fusion
  2.2 0.1 compare_select_fusion
  2.3 1.3 select_reduce_fusion
  3.6 0.0 copy-start
  3.6 0.1 slice.3
  3.7 0.5 fusion.3.span_ref
  4.2 0.3 multiply_cosine_fusion
  4.5 0.7 pad_maximum_fusion.rot_ref
  5.2 0.0 copy-done
  5.2 42.7 %attention_layer.1 = (bf16[128,512]{1,0:T(8,128)(2,1)}, bf16[128,512]{1,0:T(8,128)(2,1)}, bf16[128,4096]{1,0:T(8,128)(2,1)}, bf16[128,4224]{1,0:T(8,128)(2,1)}, f32[128,128]{1,0:T(8,128)}) custom-call(s32[128]{0:T(128)} %get-tuple-element.18.order_ref, s32[128]{0:T(128)} %copy-done, s32[16]{0:T(128)} %fusion.3.span_ref, bf16[128,4096]{1,0:T(8,128)(2,1)} %x_ref.1, ...), custom_call_target="tpu_custom_call" | custom-call | tf_op jit(solution)/shard_map/attention_layer/pallas_call | solution.py:211
  47.9 1.6 reshape.169
  49.5 1.6 reshape.170
  51.1 72.6 %gather_rows.1 = (bf16[8,256,448]{2,1,0:T(8,128)(2,1)}, s32[8,128,128]{2,1,0:T(8,128)}) custom-call(bf16[128,4224]{1,0:T(8,128)(2,1)} %get-tuple-element.10.h_ref, bf16[448,4096]{1,0:T(8,128)(2,1)} %bitcast.23, bf16[448,4096]{1,0:T(8,128)(2,1)} %bitcast.24), custom_call_target="tpu_custom_call" | custom-call | tf_op jit(solution)/shard_map/gather_rows/pallas_call | solution.py:486
  123.7 122.0 %return_rows.1 = bf16[128,4096]{1,0:T(8,128)(2,1)} custom-call(bf16[8,256,448]{2,1,0:T(8,128)(2,1)} %get-tuple-element.11.z_ref, bf16[448,4096]{1,0:T(8,128)(2,1)} %bitcast.25, s32[8,128,128]{2,1,0:T(8,128)} %get-tuple-element.12.rel_ref, f32[128,128]{1,0:T(8,128)} %get-tuple-element.13.gate_ref, bf16[128,4096]{1,0:T(8,128)(2,1)} %get-tuple-element.14.x_ref), custom_call_target="tpu_custom_call" | custom-call | tf_op jit(solution)/shard_map/return_rows/pallas_call | solution.py:505
  245.7 2.3 copy.27
  (1 shorter events, 0.0 us)
Async XLA Ops:
  3.6 1.6 copy-start

commit v6 on v5

--- a/solution.py
+++ b/solution.py
@@ -20,7 +20,7 @@
 TILE = 512
 HALF = 2048
 GROUP = 8
-PART = 4
+PART = 8
 DEPTH = 3
 CHUNK = 64
 
@@ -37,7 +37,7 @@
 
 
 def attend_kernel(kv_heads, order_ref, pos_ref, span_ref, x_ref, g1_ref, c1_ref, g2_ref, c2_ref, bo_ref, bq_ref, bk_ref, bv_ref, rot_ref, elig_ref, one_ref, two_ref, wr_ref, wq_hbm, wk_hbm, wv_hbm, wo_hbm, k_hbm, v_hbm,
-                  k_out, v_out, x_out, h_out, gate_out, w_buf, k_buf, v_buf, q_all, kn_all, vn_all, o_all, h_buf, where_ref, w_sem, o_sem, kv_sem):
+                  k_out, v_out, x_out, h_out, gate_out, w_buf, k_buf, v_buf, q_all, kn_all, vn_all, o_all, new_all, h_buf, where_ref, w_sem, o_sem, kv_sem):
     rows, d_model = x_ref.shape
     heads = q_all.shape[1]
     share = heads // kv_heads
@@ -100,15 +100,18 @@
     lin = product(q_tiles, row_of(bk_ref))
     for n in range(kv_heads):
         val = turned(lin[:, n * LANES:(n + 1) * LANES])
-        k_out[:, n * LANES:(n + 1) * LANES] = val
+        new_all[:, n, :] = val.astype(jnp.float32)
         for m in range(share):
             kn_all[:, n * share + m, :] = val.astype(jnp.float32)
+    k_out[...] = new_all[...].astype(jnp.bfloat16)
     lin = product(q_tiles + 1, row_of(bv_ref))
     for n in range(kv_heads):
         val = lin[:, n * LANES:(n + 1) * LANES].astype(jnp.bfloat16)
-        v_out[:, n * LANES:(n + 1) * LANES] = val
+        new_all[:, n, :] = val.astype(jnp.float32)
         for m in range(share):
             vn_all[:, n * share + m, :] = val.astype(jnp.float32)
+
+    v_out[...] = new_all[...].astype(jnp.bfloat16)
 
     def out_weights(tile):
         return pltpu.make_async_copy(wo_hbm.at[:, pl.ds(tile * TILE, TILE)], w_buf.at[tile], o_sem.at[tile])
@@ -211,7 +214,7 @@
     return pl.pallas_call(
         functools.partial(attend_kernel, kv_heads),
         name='attention_layer',
-        out_shape=(jax.ShapeDtypeStruct((rows, kv_dim), jnp.bfloat16), jax.ShapeDtypeStruct((rows, kv_dim), jnp.bfloat16),
+        out_shape=(jax.ShapeDtypeStruct((rows, kv_heads, head_dim), jnp.bfloat16), jax.ShapeDtypeStruct((rows, kv_heads, head_dim), jnp.bfloat16),
                    jax.ShapeDtypeStruct((rows, d_model), jnp.bfloat16), jax.ShapeDtypeStruct((rows, d_model + LANES), jnp.bfloat16),
                    jax.ShapeDtypeStruct((rows, LANES), jnp.float32)),
         in_specs=[smem, smem, smem] + [vmem] * 14 + [hbm, hbm, hbm, hbm, hbm, hbm],
@@ -220,6 +223,7 @@
             pltpu.VMEM((2 * (heads * head_dim + 2 * kv_dim) // TILE, HALF, TILE), jnp.bfloat16),
             pltpu.VMEM((DEPTH, GROUP) + flat[1:], jnp.bfloat16), pltpu.VMEM((DEPTH, GROUP) + flat[1:], jnp.bfloat16),
             spread, spread, spread, spread,
+            pltpu.VMEM((rows, kv_heads, head_dim), jnp.float32),
             pltpu.VMEM((rows, d_model), jnp.bfloat16),
             pltpu.VMEM((PART * heads, flat[1]), jnp.int32),
             pltpu.SemaphoreType.DMA((2 * (heads * head_dim + 2 * kv_dim) // TILE,)),
@@ -351,9 +355,12 @@
             hop(f, 0, slot).wait_send()
 
 
-def return_kernel(z_ref, wd_ref, rel_ref, gate_ref, x_ref, out_ref, pair_buf, side_buf, near_buf, turn_buf, turn_in, last_buf, last_in, side_send, side_recv, hop_send, hop_recv):
+def return_kernel(z_hbm, wd_hbm, rel_ref, gate_ref, x_hbm, out_ref, z_ref, wd_ref, x_ref, in_sem, pair_buf, side_buf, near_buf, turn_buf, turn_in, last_buf, last_in, side_send, side_recv, hop_send, hop_recv):
     rows = x_ref.shape[0]
     chunks = pair_buf.shape[0]
+    loads = [pltpu.make_async_copy(src, dst, in_sem.at[i]) for i, (src, dst) in enumerate(((z_hbm, z_ref), (wd_hbm, wd_ref), (x_hbm, x_ref)))]
+    for copy in loads:
+        copy.start()
     me = meet_neighbours()
 
     def slot_of(f, place):
@@ -451,6 +458,8 @@
         for part in tail:
             step(part)
 
+    for copy in loads[:2]:
+        copy.wait()
     for f in range(3):
         project(body(f, 0))
 
@@ -466,6 +475,7 @@
         send_far(part)
     sweep(turn)
     sweep(last)
+    loads[2].wait()
     sweep(finish)
 
     def drain(part):
@@ -487,7 +497,7 @@
         functools.partial(gather_kernel, bounds),
         name='gather_rows',
         out_shape=(jax.ShapeDtypeStruct((8, 2 * rows, d_ff), jnp.bfloat16), jax.ShapeDtypeStruct((8, rows, LANES), jnp.int32)),
-        in_specs=[pl.BlockSpec(memory_space=pl.ANY)] * 3,
+        in_specs=[pl.BlockSpec(memory_space=pltpu.HBM)] * 3,
         out_specs=(vmem, vmem),
         scratch_shapes=[pltpu.VMEM((8, 2 * rows, hi - lo), jnp.bfloat16) for lo, hi in bounds] + [
             pltpu.VMEM(w_gate.shape, jnp.bfloat16), pltpu.VMEM(w_gate.shape, jnp.bfloat16),
@@ -501,14 +511,16 @@
 def project_and_return(z_val, w_down, rel, gates, x_mid):
     rows, d_model = x_mid.shape
     chunks = d_model // WIDTH
+    hbm = pl.BlockSpec(memory_space=pltpu.HBM)
     vmem = pl.BlockSpec(memory_space=pltpu.VMEM)
     return pl.pallas_call(
         return_kernel,
         name='return_rows',
         out_shape=jax.ShapeDtypeStruct((rows, d_model), jnp.bfloat16),
-        in_specs=[vmem] * 5,
+        in_specs=[hbm, hbm, vmem, vmem, hbm],
         out_specs=vmem,
         scratch_shapes=[
+            pltpu.VMEM(z_val.shape, jnp.bfloat16), pltpu.VMEM(w_down.shape, jnp.bfloat16), pltpu.VMEM(x_mid.shape, jnp.bfloat16), pltpu.SemaphoreType.DMA((3,)),
             pltpu.VMEM((chunks, 2, 8 * rows, WIDTH), jnp.bfloat16),
             pltpu.VMEM((chunks, 8 * rows, WIDTH), jnp.bfloat16),
             pltpu.VMEM((chunks, 2, 4 * rows, WIDTH), jnp.bfloat16),
@@ -524,11 +536,9 @@
 
 def solution(mesh):
     def local_step(tokens, k_cache, v_cache, positions, expert_one, expert_two, eligible, ln1_gain, ln1_bias, w_query, b_query, w_key, b_key, w_value, b_value, w_out, b_out, ln2_gain, ln2_bias, w_router, w_gate, w_up, w_down):
-        rows, seq_len, kv_heads, head_dim = k_cache.shape
-        k_val, v_val, x_mid, h_ext, gates = attention_layer(tokens, k_cache, v_cache, positions, expert_one, expert_two, eligible, ln1_gain, ln1_bias, w_query, b_query, w_key, b_key, w_value, b_value, w_out, b_out, ln2_gain, ln2_bias, w_router)
+        key_new, value_new, x_mid, h_ext, gates = attention_layer(tokens, k_cache, v_cache, positions, expert_one, expert_two, eligible, ln1_gain, ln1_bias, w_query, b_query, w_key, b_key, w_value, b_value, w_out, b_out, ln2_gain, ln2_bias, w_router)
         z_val, rel = gather_and_activate(h_ext, w_gate[0].T, w_up[0].T)
         tokens_out = project_and_return(z_val, w_down[0], rel, gates, x_mid)
-        key_new, value_new = k_val.reshape(rows, kv_heads, head_dim), v_val.reshape(rows, kv_heads, head_dim)
         return tokens_out, key_new, value_new
 
     row_spec = P('ep', None)

time: 248 us -> 241 us (0.972)
  local copies, waits for them, and re-layouts: 5.58 us -> 2.39 us
  Pallas kernels: 237 us -> 234 us
    pallas_call x1, Pallas kernels: 42.7 us -> 39.4 us  [attention_layer(): pl.pallas_call(functools.partial(attend_kernel, kv_heads), name='attentio...]
    reshape x2 -> x0, local copies, waits for them, and re-layouts: 3.19 us -> none  [the longest x1 1.59 us: local_step(): k_val.reshape(rows, kv_heads, head_dim)]
where the time goes in v6:
time: 241 us
  Pallas kernels  234 us (97%)
  other arithmetic  4.48 us (2%)
    pallas_call x1, Pallas kernels, project_and_return(): pl.pallas_call(return_kernel, name='return_rows', out_shape=jax.ShapeDtyp...  122 us
    pallas_call x1, Pallas kernels, gather_and_activate(): pl.pallas_call(functools.partial(gather_kernel, bounds), name='gather_row...  72.2 us
    pallas_call x1, Pallas kernels, attention_layer(): pl.pallas_call(functools.partial(attend_kernel, kv_heads), name='attentio...  39.4 us

profile of v6, /device:TPU:0, one launch (start us, length us, event | category | flops | bytes accessed | tf_op | source)
XLA Modules:
  0.0 241.3 jit_solution(12991929775093756736)
XLA Ops:
  0.6 0.7 convert_element_type.7
  1.3 0.9 convert_reduce_fusion
  2.2 0.1 compare_select_fusion
  2.3 1.4 select_reduce_fusion
  3.7 0.0 copy-start
  3.7 0.1 slice.3
  3.8 0.5 fusion.3.span_ref
  4.3 0.3 multiply_cosine_fusion
  4.6 0.6 pad_maximum_fusion.rot_ref
  5.2 0.0 copy-done
  5.2 39.4 %attention_layer.1 = (bf16[128,4,128]{2,1,0:T(4,128)(2,1)}, bf16[128,4,128]{2,1,0:T(4,128)(2,1)}, bf16[128,4096]{1,0:T(8,128)(2,1)}, bf16[128,4224]{1,0:T(8,128)(2,1)}, f32[128,128]{1,0:T(8,128)}) custom-call(s32[128]{0:T(128)} %get-tuple-element.18.order_ref, s32[128]{0:T(128)} %copy-done, s32[16]{0:T(128)} %fusion.3.span_ref, bf16[128,4096]{1,0:T(8,128)(2,1)} %x_ref.1, ...), custom_call_target="tpu_custom_call" | custom-call | tf_op jit(solution)/shard_map/attention_layer/pallas_call | solution.py:214
  44.6 72.2 %gather_rows.1 = (bf16[8,256,448]{2,1,0:T(8,128)(2,1)}, s32[8,128,128]{2,1,0:T(8,128)}) custom-call(bf16[128,4224]{1,0:T(8,128)(2,1)} %get-tuple-element.10.h_ref, bf16[448,4096]{1,0:T(8,128)(2,1)} %bitcast.23, bf16[448,4096]{1,0:T(8,128)(2,1)} %bitcast.24), custom_call_target="tpu_custom_call" | custom-call | tf_op jit(solution)/shard_map/gather_rows/pallas_call | solution.py:496
  116.9 122.1 %return_rows.1 = bf16[128,4096]{1,0:T(8,128)(2,1)} custom-call(bf16[8,256,448]{2,1,0:T(8,128)(2,1)} %get-tuple-element.11.z_hbm, bf16[448,4096]{1,0:T(8,128)(2,1)} %bitcast.25, s32[8,128,128]{2,1,0:T(8,128)} %get-tuple-element.12.rel_ref, f32[128,128]{1,0:T(8,128)} %get-tuple-element.13.gate_ref, bf16[128,4096]{1,0:T(8,128)(2,1)} %get-tuple-element.14.x_hbm), custom_call_target="tpu_custom_call" | custom-call | tf_op jit(solution)/shard_map/return_rows/pallas_call | solution.py:516
  239.0 2.3 copy.27
  (1 shorter events, 0.0 us)
Async XLA Ops:
  3.7 1.6 copy-start

commit v7 on v6

--- a/solution.py
+++ b/solution.py
@@ -21,7 +21,7 @@
 HALF = 2048
 GROUP = 8
 PART = 8
-DEPTH = 3
+DEPTH = 4
 CHUNK = 64
 
 
@@ -36,7 +36,7 @@
     return centered * lax.rsqrt(var_val + LN_EPS) * gain + bias
 
 
-def attend_kernel(kv_heads, order_ref, pos_ref, span_ref, x_ref, g1_ref, c1_ref, g2_ref, c2_ref, bo_ref, bq_ref, bk_ref, bv_ref, rot_ref, elig_ref, one_ref, two_ref, wr_ref, wq_hbm, wk_hbm, wv_hbm, wo_hbm, k_hbm, v_hbm,
+def attend_kernel(kv_heads, order_ref, pos_ref, x_ref, g1_ref, c1_ref, g2_ref, c2_ref, bo_ref, bq_ref, bk_ref, bv_ref, cos_ref, sin_ref, elig_ref, one_ref, two_ref, wr_ref, wq_hbm, wk_hbm, wv_hbm, wo_hbm, k_hbm, v_hbm,
                   k_out, v_out, x_out, h_out, gate_out, w_buf, k_buf, v_buf, q_all, kn_all, vn_all, o_all, new_all, h_buf, where_ref, w_sem, o_sem, kv_sem):
     rows, d_model = x_ref.shape
     heads = q_all.shape[1]
@@ -63,8 +63,9 @@
             yield pltpu.make_async_copy(v_hbm.at[t, pl.ds(0, size)], v_buf.at[slot, j, pl.ds(0, size)], kv_sem.at[slot, 1])
 
     def each_span(g, body):
+        span = jnp.clip(lax.div(pos_ref[g * GROUP] + (CHUNK - 1), CHUNK), 1, spans)
         for n in range(1, spans + 1):
-            @pl.when(span_ref[g] == n)
+            @pl.when(span == n)
             def _(n=n):
                 body(n)
 
@@ -90,7 +91,7 @@
         return lin + bias
 
     def turned(head):
-        return (head * rot_ref[0] + pltpu.roll(head, LANES // 2, 1) * rot_ref[1]).astype(jnp.bfloat16)
+        return (head * cos_ref[...] + pltpu.roll(head, LANES // 2, 1) * sin_ref[...]).astype(jnp.bfloat16)
 
     bq_row = row_of(bq_ref)
     for i in range(q_tiles):
@@ -114,10 +115,9 @@
     v_out[...] = new_all[...].astype(jnp.bfloat16)
 
     def out_weights(tile):
-        return pltpu.make_async_copy(wo_hbm.at[:, pl.ds(tile * TILE, TILE)], w_buf.at[tile], o_sem.at[tile])
-
-    for tile in range(d_model // TILE):
-        out_weights(tile).start()
+        return pltpu.make_async_copy(wo_hbm.at[:, pl.ds(pl.multiple_of(tile * TILE, TILE), TILE)], w_buf.at[tile], o_sem.at[tile])
+
+    stride = groups // (d_model // TILE)
 
     block = lax.broadcasted_iota(jnp.int32, (PART * heads, 1), 0) // heads
 
@@ -126,6 +126,10 @@
         @pl.when(g + DEPTH - 1 < groups)
         def _():
             fetch(g + DEPTH - 1)
+
+        @pl.when(lax.rem(g, stride) == 0)
+        def _():
+            out_weights(lax.div(g, stride)).start()
 
         slot = lax.rem(g, DEPTH)
 
@@ -161,7 +165,7 @@
 
     bo_row = row_of(bo_ref)
     for tile in range(d_model // TILE):
-        out_weights(tile).wait()
+        out_weights(jnp.int32(tile)).wait()
         at = slice(tile * TILE, (tile + 1) * TILE)
         acc = jnp.dot(h_buf[:, :heads * LANES], w_buf[tile], preferred_element_type=jnp.float32)
         x_out[:, at] = (x_ref[:, at].astype(jnp.float32) + acc + bo_row[:, at]).astype(jnp.bfloat16)
@@ -194,17 +198,15 @@
     heads = w_query.shape[1] // head_dim
     kv_dim = kv_heads * head_dim
     ids = jnp.arange(rows, dtype=jnp.int32)
-    ahead = (positions[None, :] < positions[:, None]) | ((positions[None, :] == positions[:, None]) & (ids[None, :] < ids[:, None]))
+    ahead = (positions[None, :] > positions[:, None]) | ((positions[None, :] == positions[:, None]) & (ids[None, :] < ids[:, None]))
     rank = jnp.sum(ahead.astype(jnp.int32), axis=1)
     hit = rank[None, :] == ids[:, None]
     order = jnp.sum(jnp.where(hit, ids[None, :], 0), axis=1)
     pos_sorted = jnp.sum(jnp.where(hit, positions[None, :], 0), axis=1)
-    span = jnp.clip((pos_sorted[GROUP - 1::GROUP] + CHUNK - 1) // CHUNK, 1, seq_len // CHUNK)
     half_dim = head_dim // 2
     inv_freq = ROPE_BASE ** (jnp.arange(half_dim, dtype=jnp.float32) * (-2.0 / head_dim))
     angles = positions.astype(jnp.float32)[:, None] * jnp.concatenate([inv_freq, inv_freq])[None, :]
     sign = jnp.where(jnp.arange(head_dim) < half_dim, -1.0, 1.0).astype(jnp.float32)
-    rot = jnp.stack([jnp.cos(angles), jnp.sin(angles) * sign[None, :]])
     small = [p.reshape(-1, LANES) for p in (ln1_gain, ln1_bias, ln2_gain, ln2_bias, b_out, b_query, b_key, b_value)]
     vmem = pl.BlockSpec(memory_space=pltpu.VMEM)
     smem = pl.BlockSpec(memory_space=pltpu.SMEM)
@@ -217,7 +219,7 @@
         out_shape=(jax.ShapeDtypeStruct((rows, kv_heads, head_dim), jnp.bfloat16), jax.ShapeDtypeStruct((rows, kv_heads, head_dim), jnp.bfloat16),
                    jax.ShapeDtypeStruct((rows, d_model), jnp.bfloat16), jax.ShapeDtypeStruct((rows, d_model + LANES), jnp.bfloat16),
                    jax.ShapeDtypeStruct((rows, LANES), jnp.float32)),
-        in_specs=[smem, smem, smem] + [vmem] * 14 + [hbm, hbm, hbm, hbm, hbm, hbm],
+        in_specs=[smem, smem] + [vmem] * 15 + [hbm, hbm, hbm, hbm, hbm, hbm],
         out_specs=(vmem,) * 5,
         scratch_shapes=[
             pltpu.VMEM((2 * (heads * head_dim + 2 * kv_dim) // TILE, HALF, TILE), jnp.bfloat16),
@@ -230,7 +232,7 @@
             pltpu.SemaphoreType.DMA((d_model // TILE,)),
             pltpu.SemaphoreType.DMA((DEPTH, 2))],
         compiler_params=pltpu.CompilerParams(vmem_limit_bytes=62 * 1024 * 1024),
-    )(order, pos_sorted, span, tokens, *small, rot, eligible.T, expert_one[None], expert_two[None], w_router.T, w_query, w_key, w_value, w_out, k_cache.reshape(flat), v_cache.reshape(flat))
+    )(order, pos_sorted, tokens, *small, jnp.cos(angles), jnp.sin(angles) * sign[None, :], eligible.T, expert_one[None], expert_two[None], w_router.T, w_query, w_key, w_value, w_out, k_cache.reshape(flat), v_cache.reshape(flat))
 
 
 def seat(slot):
@@ -275,20 +277,19 @@
     def landed(f, slot):
         hop(f, 0, slot).wait_recv()
 
-    def activate(first, count):
+    def activate(place):
         u_val = v_val = None
         for f in range(3):
             lo, hi = bounds[f]
             hi = min(hi, wg_ref.shape[1])
-            x_val = bufs[f][first:first + count, :, : hi - lo].reshape(2 * rows * count, hi - lo)
+            x_val = bufs[f][place, :, : hi - lo]
             u_part = lax.dot_general(x_val, wg_ref[:, lo:hi], ALONG, preferred_element_type=jnp.float32)
             v_part = lax.dot_general(x_val, wu_ref[:, lo:hi], ALONG, preferred_element_type=jnp.float32)
             u_val = u_part if u_val is None else u_val + u_part
             v_val = v_part if v_val is None else v_val + v_part
-        z_ref[first:first + count] = (jax.nn.silu(u_val) * v_val).astype(jnp.bfloat16).reshape(count, 2 * rows, -1)
-        for i in range(first, first + count):
-            ids = bufs[2][i, :rows, bounds[2][1] - bounds[2][0] - LANES:]
-            rel_ref[i] = ids.astype(jnp.float32).astype(jnp.int32) ^ me
+        z_ref[place] = (jax.nn.silu(u_val) * v_val).astype(jnp.bfloat16)
+        ids = bufs[2][place, :rows, bounds[2][1] - bounds[2][0] - LANES:]
+        rel_ref[place] = ids.astype(jnp.float32).astype(jnp.int32) ^ me
 
     for f in range(3):
         copies[f].wait()
@@ -305,7 +306,7 @@
         side(f, 0).wait_recv()
     for copy in weights:
         copy.wait()
-    activate(0, 1)
+    activate(0)
     for f in range(3):
         a, b, g = ORDERS[f]
         landed(f, a)
@@ -330,7 +331,7 @@
         for slot in (1, 2, 4):
             side(f, slot).wait_recv()
 
-    activate(1, 3)
+    pl.loop(1, 4)(activate)
     for f in range(3):
         a, b, g = ORDERS[f]
         landed(f, a ^ g)
@@ -341,13 +342,13 @@
         for slot in (3, 5, 6):
             side(f, slot).wait_recv()
 
-    activate(4, 3)
+    pl.loop(4, 7)(activate)
     for f in range(3):
         landed(f, 7)
         side(f, 7).start()
     for f in range(3):
         side(f, 7).wait_recv()
-    activate(7, 1)
+    activate(7)
     for f in range(3):
         for slot in range(8):
             side(f, slot).wait_send()

time: 241 us -> 239 us (level)
  no operation moved by 1% of the time
where the time goes in v7:
time: 239 us
  Pallas kernels  232 us (97%)
  other arithmetic  3.95 us (2%)
    pallas_call x1, Pallas kernels, project_and_return(): pl.pallas_call(return_kernel, name='return_rows', out_shape=jax.ShapeDtyp...  122 us
    pallas_call x1, Pallas kernels, gather_and_activate(): pl.pallas_call(functools.partial(gather_kernel, bounds), name='gather_row...  73 us
    pallas_call x1, Pallas kernels, attention_layer(): pl.pallas_call(functools.partial(attend_kernel, kv_heads), name='attentio...  37 us

profile of v7, /device:TPU:0, one launch (start us, length us, event | category | flops | bytes accessed | tf_op | source)
XLA Modules:
  0.0 239.4 jit_solution(4664084736841097193)
XLA Ops:
  0.6 0.7 convert_element_type.7
  1.3 0.9 convert_reduce_fusion
  2.2 0.1 compare_select_fusion
  2.3 1.3 select_reduce_fusion
  3.6 1.0 fusion
  4.6 37.0 %attention_layer.1 = (bf16[128,4,128]{2,1,0:T(4,128)(2,1)}, bf16[128,4,128]{2,1,0:T(4,128)(2,1)}, bf16[128,4096]{1,0:T(8,128)(2,1)}, bf16[128,4224]{1,0:T(8,128)(2,1)}, f32[128,128]{1,0:T(8,128)}) custom-call(s32[128]{0:T(128)} %get-tuple-element.18.order_ref, s32[128]{0:T(128)} %get-tuple-element.17.pos_ref, bf16[128,4096]{1,0:T(8,128)(2,1)} %x_ref.1, ...), custom_call_target="tpu_custom_call" | custom-call | tf_op jit(solution)/shard_map/attention_layer/pallas_call | solution.py:216
  41.6 73.0 %gather_rows.1 = (bf16[8,256,448]{2,1,0:T(8,128)(2,1)}, s32[8,128,128]{2,1,0:T(8,128)}) custom-call(bf16[128,4224]{1,0:T(8,128)(2,1)} %get-tuple-element.10.h_ref, bf16[448,4096]{1,0:T(8,128)(2,1)} %bitcast.23, bf16[448,4096]{1,0:T(8,128)(2,1)} %bitcast.24), custom_call_target="tpu_custom_call" | custom-call | tf_op jit(solution)/shard_map/gather_rows/pallas_call | solution.py:497
  114.6 122.5 %return_rows.1 = bf16[128,4096]{1,0:T(8,128)(2,1)} custom-call(bf16[8,256,448]{2,1,0:T(8,128)(2,1)} %get-tuple-element.11.z_hbm, bf16[448,4096]{1,0:T(8,128)(2,1)} %bitcast.25, s32[8,128,128]{2,1,0:T(8,128)} %get-tuple-element.12.rel_ref, f32[128,128]{1,0:T(8,128)} %get-tuple-element.13.gate_ref, bf16[128,4096]{1,0:T(8,128)(2,1)} %get-tuple-element.14.x_hbm), custom_call_target="tpu_custom_call" | custom-call | tf_op jit(solution)/shard_map/return_rows/pallas_call | solution.py:517
  237.1 2.3 copy.27
  (1 shorter events, 0.0 us)

commit v8 on v7

--- a/solution.py
+++ b/solution.py
@@ -277,19 +277,20 @@
     def landed(f, slot):
         hop(f, 0, slot).wait_recv()
 
-    def activate(place):
+    def activate(place, count=1):
         u_val = v_val = None
+        span = pl.ds(place, count)
         for f in range(3):
             lo, hi = bounds[f]
             hi = min(hi, wg_ref.shape[1])
-            x_val = bufs[f][place, :, : hi - lo]
+            x_val = bufs[f][span, :, : hi - lo].reshape(2 * rows * count, hi - lo)
             u_part = lax.dot_general(x_val, wg_ref[:, lo:hi], ALONG, preferred_element_type=jnp.float32)
             v_part = lax.dot_general(x_val, wu_ref[:, lo:hi], ALONG, preferred_element_type=jnp.float32)
             u_val = u_part if u_val is None else u_val + u_part
             v_val = v_part if v_val is None else v_val + v_part
-        z_ref[place] = (jax.nn.silu(u_val) * v_val).astype(jnp.bfloat16)
-        ids = bufs[2][place, :rows, bounds[2][1] - bounds[2][0] - LANES:]
-        rel_ref[place] = ids.astype(jnp.float32).astype(jnp.int32) ^ me
+        z_ref[span] = (jax.nn.silu(u_val) * v_val).astype(jnp.bfloat16).reshape(count, 2 * rows, -1)
+        ids = bufs[2][span, :rows, bounds[2][1] - bounds[2][0] - LANES:]
+        rel_ref[span] = ids.astype(jnp.float32).astype(jnp.int32) ^ me
 
     for f in range(3):
         copies[f].wait()
@@ -331,7 +332,10 @@
         for slot in (1, 2, 4):
             side(f, slot).wait_recv()
 
-    pl.loop(1, 4)(activate)
+    @pl.loop(1, 4)
+    def _(place):
+        activate(place)
+
     for f in range(3):
         a, b, g = ORDERS[f]
         landed(f, a ^ g)
@@ -342,7 +346,7 @@
         for slot in (3, 5, 6):
             side(f, slot).wait_recv()
 
-    pl.loop(4, 7)(activate)
+    activate(4, 3)
     for f in range(3):
         landed(f, 7)
         side(f, 7).start()

time: 239 us -> 239 us (level)
  no operation moved by 1% of the time
where the time goes in v8:
time: 239 us
  Pallas kernels  232 us (97%)
  other arithmetic  3.95 us (2%)
    pallas_call x1, Pallas kernels, project_and_return(): pl.pallas_call(return_kernel, name='return_rows', out_shape=jax.ShapeDtyp...  123 us
    pallas_call x1, Pallas kernels, gather_and_activate(): pl.pallas_call(functools.partial(gather_kernel, bounds), name='gather_row...  72.7 us
    pallas_call x1, Pallas kernels, attention_layer(): pl.pallas_call(functools.partial(attend_kernel, kv_heads), name='attentio...  37.2 us

profile of v8, /device:TPU:0, one launch (start us, length us, event | category | flops | bytes accessed | tf_op | source)
XLA Modules:
  0.0 239.4 jit_solution(2215301624052064656)
XLA Ops:
  0.6 0.7 convert_element_type.7
  1.3 0.9 convert_reduce_fusion
  2.2 0.1 compare_select_fusion
  2.3 1.3 select_reduce_fusion
  3.6 1.0 fusion
  4.6 37.2 %attention_layer.1 = (bf16[128,4,128]{2,1,0:T(4,128)(2,1)}, bf16[128,4,128]{2,1,0:T(4,128)(2,1)}, bf16[128,4096]{1,0:T(8,128)(2,1)}, bf16[128,4224]{1,0:T(8,128)(2,1)}, f32[128,128]{1,0:T(8,128)}) custom-call(s32[128]{0:T(128)} %get-tuple-element.18.order_ref, s32[128]{0:T(128)} %get-tuple-element.17.pos_ref, bf16[128,4096]{1,0:T(8,128)(2,1)} %x_ref.1, ...), custom_call_target="tpu_custom_call" | custom-call | tf_op jit(solution)/shard_map/attention_layer/pallas_call | solution.py:216
  41.8 72.7 %gather_rows.1 = (bf16[8,256,448]{2,1,0:T(8,128)(2,1)}, s32[8,128,128]{2,1,0:T(8,128)}) custom-call(bf16[128,4224]{1,0:T(8,128)(2,1)} %get-tuple-element.10.h_ref, bf16[448,4096]{1,0:T(8,128)(2,1)} %bitcast.23, bf16[448,4096]{1,0:T(8,128)(2,1)} %bitcast.24), custom_call_target="tpu_custom_call" | custom-call | tf_op jit(solution)/shard_map/gather_rows/pallas_call | solution.py:501
  114.4 122.7 %return_rows.1 = bf16[128,4096]{1,0:T(8,128)(2,1)} custom-call(bf16[8,256,448]{2,1,0:T(8,128)(2,1)} %get-tuple-element.11.z_hbm, bf16[448,4096]{1,0:T(8,128)(2,1)} %bitcast.25, s32[8,128,128]{2,1,0:T(8,128)} %get-tuple-element.12.rel_ref, f32[128,128]{1,0:T(8,128)} %get-tuple-element.13.gate_ref, bf16[128,4096]{1,0:T(8,128)(2,1)} %get-tuple-element.14.x_hbm), custom_call_target="tpu_custom_call" | custom-call | tf_op jit(solution)/shard_map/return_rows/pallas_call | solution.py:521
  237.1 2.3 copy.27
  (1 shorter events, 0.0 us)
